TPU v7x, 256 devices: a whole 4x4x8 slice. The times are simulated.
256 devices in a mesh: frame: 32 (over y_hi, z, core), stream: 8 (over y_lo, x).
Axes of the slice: x: 4, y: 4 (y_hi: 2, y_lo: 2; y = y_hi * 2 + y_lo), z: 8, core: 2. Of those that a mesh axis runs over, the one named last changes fastest.
Arguments:
- query: bfloat16 [8, 4096, 4096], P('stream', 'frame'), may hold values from -60 to 60
- key: bfloat16 [8, 4096, 4096], P('stream', 'frame'), may hold values from -4 to 4
- value: bfloat16 [8, 4096, 4096], P('stream', 'frame'), may hold values from -24 to 24
- latent: bfloat16 [8, 4096, 4096], P('stream', 'frame'), may hold values from -6 to 6
- target: bfloat16 [8, 4096, 4096], P('stream', 'frame'), may hold values from -6 to 6
- noise_level: float32 [8, 16], P('stream'), may hold values from 0.02 to 0.98
- mod_weight: bfloat16 [4096, 256], replicated, may hold values from -0.375 to 0.375
- block_order: int32 [64], replicated, may hold values from 0 to 63, as said below
- context_start: int32 [8, 16], P('stream'), may hold values from 0 to 15, as said below
Outputs:
- grad_weight: float32 [4096, 256], P('frame')
Inputs may be any that keep to these rules, and one draw needn't show every extreme that they name: block_order is a permutation of 0 to 63, and entries 2 i and 2 i + 1 add up to 63. context_start[s, c] lies between 0 and c.
All inputs are finite; a program needn't handle non-finite values.
Results may differ from a plain program's by a relative error of at most 0.0016.
Values may be sent and summed in bfloat16 or wider, within the bound.
No kernel may reach another device: no remote copies, remote signals or barrier semaphores. Data moves between devices by JAX's collectives and lax.ppermute only.
A program may use at most 64 MiB of HBM per device.

v0:
```python
import functools
import math

import jax
import jax.numpy as jnp
from jax import lax
from jax.experimental import pallas as pl
from jax.experimental.pallas import tpu as pltpu
from jax.sharding import PartitionSpec as P

HEAD_DIM = 128
CHUNK = 4


def panels_kernel(*refs, panel):
    ins, out = refs[:-1], refs[-1]
    rows = ins[0].shape[0]
    for k in range(out.shape[0]):
        for a, ref in enumerate(ins):
            out[k, a * rows : (a + 1) * rows, :] = ref[:, k * panel : (k + 1) * panel]


def difference_kernel(latent, target, out, *, panel):
    for k in range(out.shape[0]):
        part = slice(k * panel, (k + 1) * panel)
        wide = latent[:, part].astype(jnp.float32) - target[:, part].astype(jnp.float32)
        out[k] = wide.astype(jnp.bfloat16)


def to_panels(kernel, arrays, frames, stacked):
    rows, width = arrays[0].shape
    panel = width // frames
    step = max(1, frames // 4)
    return pl.pallas_call(
        functools.partial(kernel, panel=panel),
        grid=(frames // step,),
        in_specs=[pl.BlockSpec((rows, step * panel), lambda i: (0, i))] * len(arrays),
        out_specs=pl.BlockSpec((step, stacked * rows, panel), lambda i: (i, 0, 0)),
        out_shape=jax.ShapeDtypeStruct((frames, stacked * rows, panel), jnp.bfloat16),
    )(*arrays)


def attend_kernel(
    place, start, qkv, gate, attn_out, square_out, q_sorted, k_sorted, v_sorted, strip, *, per_group, groups
):
    block_len, dim = qkv.shape[1], qkv.shape[2]
    blocks = per_group * groups
    rows = per_group * block_len
    scale = 1.0 / math.sqrt(dim)

    def sort_block(t, carry):
        p = place[t]
        base = (p // 2) * 6 + p % 2
        at = pl.ds(pl.multiple_of(t * block_len, block_len), block_len)
        q_sorted[at, :] = qkv[base]
        k_sorted[at, :] = qkv[base + 2]
        v_sorted[at, :] = qkv[base + 4]
        return carry

    lax.fori_loop(0, blocks, sort_block, 0, unroll=8)
    pad = jnp.zeros(((CHUNK - 1) * rows, dim), jnp.bfloat16)
    k_sorted[blocks * block_len :, :] = pad
    v_sorted[blocks * block_len :, :] = pad

    def one_group(c, carry):
        first = start[c]
        count = c - first + 1
        chunks = (count + CHUNK - 1) // CHUNK
        at_q = pl.ds(pl.multiple_of(c * rows, rows), rows)
        q = q_sorted[at_q, :]

        def scores(i, peak):
            for u in range(CHUNK):
                g = first + i * CHUNK + u
                k = k_sorted[pl.ds(pl.multiple_of(g * rows, rows), rows), :]
                s = lax.dot_general(
                    q, k, (((1,), (1,)), ((), ())), preferred_element_type=jnp.float32
                )
                s = jnp.where(g <= c, s * scale, -jnp.inf)
                strip[i * CHUNK + u] = s
                for b in range(rows // 128):
                    peak = jnp.maximum(peak, s[:, b * 128 : (b + 1) * 128])
            return peak

        peak = lax.fori_loop(0, chunks, scores, jnp.full((rows, 128), -jnp.inf, jnp.float32))
        peak = jnp.max(peak, axis=1, keepdims=True)

        def exponents(i, total):
            for u in range(CHUNK):
                e = jnp.exp(strip[i * CHUNK + u] - peak)
                strip[i * CHUNK + u] = e
                for b in range(rows // 128):
                    total = total + e[:, b * 128 : (b + 1) * 128]
            return total

        total = lax.fori_loop(0, chunks, exponents, jnp.zeros((rows, 128), jnp.float32))
        inverse = 1.0 / jnp.sum(total, axis=1, keepdims=True)

        def weigh(i, acc):
            for u in range(CHUNK):
                g = first + i * CHUNK + u
                v = v_sorted[pl.ds(pl.multiple_of(g * rows, rows), rows), :]
                probs = (strip[i * CHUNK + u] * inverse).astype(jnp.bfloat16)
                acc = acc + lax.dot_general(
                    probs, v, (((1,), (0,)), ((), ())), preferred_element_type=jnp.float32
                )
            return acc

        acc = lax.fori_loop(0, chunks, weigh, jnp.zeros((rows, dim), jnp.float32))
        rounded = acc.astype(jnp.bfloat16)
        attn_out[at_q, :] = rounded
        wide = rounded.astype(jnp.float32)
        square_out[pl.ds(c, 1), :] = gate[pl.ds(c, 1), :] * jnp.sum(wide * wide, axis=0, keepdims=True)
        return carry

    lax.fori_loop(0, groups, one_group, 0)


def attend(place, start, qkv, gate, per_group, groups):
    block_len, dim = qkv.shape[1], qkv.shape[2]
    length = per_group * groups * block_len
    rows = per_group * block_len
    smem = pl.BlockSpec(memory_space=pltpu.SMEM)
    vmem = pl.BlockSpec(memory_space=pltpu.VMEM)
    padded = length + (CHUNK - 1) * rows
    return pl.pallas_call(
        functools.partial(attend_kernel, per_group=per_group, groups=groups),
        in_specs=[smem, smem, vmem, vmem],
        out_specs=[vmem, vmem],
        out_shape=[
            jax.ShapeDtypeStruct((length, dim), jnp.bfloat16),
            jax.ShapeDtypeStruct((groups, dim), jnp.float32),
        ],
        scratch_shapes=[
            pltpu.VMEM((length, dim), jnp.bfloat16),
            pltpu.VMEM((padded, dim), jnp.bfloat16),
            pltpu.VMEM((padded, dim), jnp.bfloat16),
            pltpu.VMEM((groups + CHUNK, rows, rows), jnp.float32),
        ],
        compiler_params=pltpu.CompilerParams(vmem_limit_bytes=40 * 1024 * 1024),
        cost_estimate=pl.CostEstimate(
            flops=4 * length * length * dim, bytes_accessed=4 * length * dim * 2, transcendentals=length * length
        ),
    )(place, start, qkv, gate)


def combine_kernel(place, attn, square, diff, out, *, per_group, groups):
    block_len, dim = diff.shape[1], diff.shape[2]

    for c in range(groups):
        acc = jnp.zeros((8, dim), jnp.float32)
        for b in range(per_group):
            t = c * per_group + b
            product = attn[t * block_len : (t + 1) * block_len, :].astype(jnp.float32) * diff[
                place[t]
            ].astype(jnp.float32)
            acc = acc + jnp.sum(product.reshape(block_len // 8, 8, dim), axis=0)
        row = jnp.sum(acc, axis=0, keepdims=True) + square[c : c + 1, :]
        for copy in range(out.shape[0]):
            out[copy, c : c + 1, :] = row


def combine(place, attn, square, diff, copies, per_group, groups):
    smem = pl.BlockSpec(memory_space=pltpu.SMEM)
    vmem = pl.BlockSpec(memory_space=pltpu.VMEM)
    return pl.pallas_call(
        functools.partial(combine_kernel, per_group=per_group, groups=groups),
        in_specs=[smem, vmem, vmem, vmem],
        out_specs=vmem,
        out_shape=jax.ShapeDtypeStruct((copies, groups, attn.shape[1]), jnp.float32),
    )(place, attn, square, diff)


def finish_kernel(sums, embed, out, *, root):
    out[...] = (
        lax.dot_general(
            sums[...],
            embed[...],
            (((0,), (0,)), ((), ())),
            precision=lax.Precision.HIGHEST,
            preferred_element_type=jnp.float32,
        )
        / root
    )


def finish(sums, embed, root):
    return pl.pallas_call(
        functools.partial(finish_kernel, root=root),
        out_shape=jax.ShapeDtypeStruct((sums.shape[1], embed.shape[1]), jnp.float32),
    )(sums, embed)


def sinusoid(noise, emb_width):
    half_width = emb_width // 2
    frequency = jnp.exp(-math.log(10000.0) * jnp.arange(half_width, dtype=jnp.float32) / half_width)
    angles = 1000.0 * noise[..., None] * frequency
    return jnp.concatenate([jnp.cos(angles), jnp.sin(angles)], -1).astype(jnp.bfloat16)


def exchange(value, axis):
    return lax.all_to_all(value, axis, split_axis=0, concat_axis=0, tiled=True)


def per_device(
    query, key, value, latent, target, noise_level, mod_weight, block_order, context_start
):
    frames = lax.axis_size("frame")
    streams = lax.axis_size("stream")
    index = lax.axis_index("frame")
    tokens, width = query.shape[1:]
    block_len = tokens // 2
    local_width = width // frames
    blocks = block_order.shape[0]
    groups = noise_level.shape[1]
    per_group = blocks // groups
    root = math.sqrt(per_group * block_len)

    noise_all = exchange(jnp.broadcast_to(noise_level[None], (streams, 1, groups)), "stream")
    embed_all = sinusoid(noise_all.reshape(streams * groups), mod_weight.shape[1])
    embed_own = sinusoid(noise_level[0], mod_weight.shape[1])
    weight_rows = lax.dynamic_slice_in_dim(mod_weight, index * local_width, local_width, 0)
    gate = lax.dot_general(
        embed_own, weight_rows, (((1,), (1,)), ((), ())), preferred_element_type=jnp.float32
    )
    times = jnp.arange(blocks, dtype=jnp.int32)
    place = jnp.sum(jnp.where(block_order[None, :] == times[:, None], times[None, :], 0), axis=1)

    qkv = to_panels(panels_kernel, (query[0], key[0], value[0]), frames, 3)
    diff = to_panels(difference_kernel, (latent[0], target[0]), frames, 1)
    qkv = exchange(qkv, "frame")
    diff = exchange(diff, "frame")
    attn, square = attend(
        place, context_start[0], qkv.reshape(frames * 6, block_len, local_width), gate, per_group, groups
    )
    sums = combine(
        place, attn, square, diff.reshape(frames * 2, block_len, local_width), streams, per_group, groups
    )
    sums = exchange(sums, "stream")
    return finish(
        sums.reshape(streams * groups, local_width), embed_all.astype(jnp.float32), root
    )


def solution(mesh):
    placed = (
        P("stream", "frame", None),
        P("stream", "frame", None),
        P("stream", "frame", None),
        P("stream", "frame", None),
        P("stream", "frame", None),
        P("stream", None),
        P(),
        P(),
        P("stream", None),
    )
    return jax.shard_map(
        per_device, mesh=mesh, in_specs=placed, out_specs=P("frame", None), check_vma=False
    )
```

profile of v0, /device:TPU:16, one launch (start us, length us, event | category | flops | bytes accessed | tf_op | source)
XLA Modules:
  0.0 151.4 jit_solution(6928989748832821879)
XLA Ops:
  0.0 0.0 copy-start
  0.0 1.4 broadcast_in_dim.12
  1.4 5.0 %all-to-all-start.3 = ((f32[8,1,16]{2,1,0:T(1,128)}), f32[8,1,16]{2,1,0:T(1,128)S(1)}, u32[]{:S(2)}, u32[]{:S(2)}) async-start(f32[8,1,16]{2,1,0:T(1,128)} %broadcast_in_dim.12), calls=%async_computation.3 | async-start | bytes 8192 | tf_op jit(solution)/shard_map/all_to_all | solution.py:202
  6.4 4.4 %shard_map.91 = bf16[32,384,128]{2,1,0:T(8,128)(2,1)} custom-call(bf16[128,4096]{1,0:T(8,128)(2,1)} %bitcast.15, bf16[128,4096]{1,0:T(8,128)(2,1)} %bitcast.16, bf16[128,4096]{1,0:T(8,128)(2,1)} %bitcast.17), custom_call_target="tpu_custom_call" | custom-call | tf_op jit(solution)/shard_map/pallas_call | solution.py:34
  10.8 1.8 %all-to-all-done.3 = f32[8,1,16]{2,1,0:T(1,128)S(1)} async-done(((f32[8,1,16]{2,1,0:T(1,128)}), f32[8,1,16]{2,1,0:T(1,128)S(1)}, u32[]{:S(2)}, u32[]{:S(2)}) %all-to-all-start.3) | async-done | bytes 544 | tf_op jit(solution)/shard_map/all_to_all | solution.py:202
  12.5 11.6 %all-to-all-start = ((bf16[32,384,128]{2,1,0:T(8,128)(2,1)}), bf16[32,384,128]{2,1,0:T(8,128)(2,1)}, u32[]{:S(2)}, u32[]{:S(2)}) async-start(bf16[32,384,128]{2,1,0:T(8,128)(2,1)} %shard_map.91), calls=%async_computation | async-start | bytes 6291456 | tf_op jit(solution)/shard_map/all_to_all | solution.py:202
  24.2 0.0 copy-start.7
  24.2 0.0 copy-start.8
  24.2 0.0 copy-start.4
  24.2 3.7 %shard_map.93 = bf16[32,128,128]{2,1,0:T(8,128)(2,1)} custom-call(bf16[128,4096]{1,0:T(8,128)(2,1)} %bitcast.13, bf16[128,4096]{1,0:T(8,128)(2,1)} %bitcast.14), custom_call_target="tpu_custom_call" | custom-call | tf_op jit(solution)/shard_map/pallas_call | solution.py:34
  27.9 67.8 %all-to-all-done = bf16[32,384,128]{2,1,0:T(8,128)(2,1)} async-done(((bf16[32,384,128]{2,1,0:T(8,128)(2,1)}), bf16[32,384,128]{2,1,0:T(8,128)(2,1)}, u32[]{:S(2)}, u32[]{:S(2)}) %all-to-all-start) | async-done | bytes 3145760 | tf_op jit(solution)/shard_map/all_to_all | solution.py:202
  95.7 8.5 %all-to-all-start.1 = ((bf16[32,128,128]{2,1,0:T(8,128)(2,1)}), bf16[32,128,128]{2,1,0:T(8,128)(2,1)S(1)}, u32[]{:S(2)}, u32[]{:S(2)}) async-start(bf16[32,128,128]{2,1,0:T(8,128)(2,1)} %shard_map.93), calls=%async_computation.1 | async-start | bytes 2097152 | tf_op jit(solution)/shard_map/all_to_all | solution.py:202
  104.2 0.0 copy-done.7
  104.2 0.1 fusion.4
  104.3 0.0 copy-done
  104.3 0.1 fusion.2.gate
  104.5 0.0 copy-done.8
  104.5 0.1 select_reduce_fusion.place
  104.6 0.0 copy-start.3
  104.6 0.1 mul.61
  104.7 0.3 fusion
  105.0 0.0 copy-done.4
  105.1 27.7 %shard_map.92 = (bf16[4096,128]{1,0:T(8,128)(2,1)S(1)}, f32[16,128]{1,0:T(8,128)S(1)}) custom-call(s32[64]{0:T(128)S(1)} %select_reduce_fusion.place, s32[16]{0:T(128)S(1)} %bitcast.11, bf16[192,64,128]{2,1,0:T(8,128)(2,1)} %bitcast.4.qkv, f32[16,128]{1,0:T(8,128)S(1)} %fusion.2.gate), custom_call_target="tpu_custom_call" | custom-call | flops 8589934592 | bytes 4194304 | tf_op jit(solution)/shard_map/pallas_call | solution.py:126
  132.7 0.0 copy-done.3
  132.7 0.0 copy-start.1
  132.8 1.0 copy-done.1
  133.7 0.0 copy-start.2
  133.7 0.6 copy-done.2
  134.3 0.0 all-to-all-done.1
  134.3 0.0 copy-start.5
  134.3 1.0 copy-done.5
  135.3 2.5 %shard_map.94 = f32[8,16,128]{2,1,0:T(8,128)} custom-call(s32[64]{0:T(128)} %copy-done.3, bf16[4096,128]{1,0:T(8,128)(2,1)} %copy-done.1, f32[16,128]{1,0:T(8,128)} %copy-done.2, bf16[64,64,128]{2,1,0:T(8,128)(2,1)} %bitcast.12), custom_call_target="tpu_custom_call" | custom-call | tf_op jit(solution)/shard_map/pallas_call | solution.py:166
  137.8 4.7 %all-to-all-start.2 = ((f32[8,16,128]{2,1,0:T(8,128)}), f32[8,16,128]{2,1,0:T(8,128)S(1)}, u32[]{:S(2)}, u32[]{:S(2)}) async-start(f32[8,16,128]{2,1,0:T(8,128)} %shard_map.94), calls=%async_computation.2 | async-start | bytes 131072 | tf_op jit(solution)/shard_map/all_to_all | solution.py:202
  142.5 0.7 maximum_convert_fusion.embed
  143.2 5.7 %all-to-all-done.2 = f32[8,16,128]{2,1,0:T(8,128)S(1)} async-done(((f32[8,16,128]{2,1,0:T(8,128)}), f32[8,16,128]{2,1,0:T(8,128)S(1)}, u32[]{:S(2)}, u32[]{:S(2)}) %all-to-all-start.2) | async-done | bytes 65568 | tf_op jit(solution)/shard_map/all_to_all | solution.py:202
  148.9 0.0 copy-start.6
  148.9 0.6 copy-done.6
  149.5 1.9 %shard_map.95 = f32[128,256]{1,0:T(8,128)} custom-call(f32[128,128]{1,0:T(8,128)} %bitcast.18, f32[128,256]{1,0:T(8,128)} %maximum_convert_fusion.embed), custom_call_target="tpu_custom_call" | custom-call | tf_op jit(solution)/shard_map/pallas_call | solution.py:188
  (3 shorter events, 0.0 us)
Async XLA Ops:
  0.0 104.3 %copy-start = (bf16[4096,256]{1,0:T(8,128)(2,1)S(1)}, bf16[4096,256]{1,0:T(8,128)(2,1)}, u32[]{:S(2)}) copy-start(bf16[4096,256]{1,0:T(8,128)(2,1)} %param.15) | copy-start | bytes 6291460
  1.4 11.1 %all-to-all-start.3 = ((f32[8,1,16]{2,1,0:T(1,128)}), f32[8,1,16]{2,1,0:T(1,128)S(1)}, u32[]{:S(2)}, u32[]{:S(2)}) async-start(f32[8,1,16]{2,1,0:T(1,128)} %broadcast_in_dim.12), calls=%async_computation.3 | async-start | bytes 8192 | tf_op jit(solution)/shard_map/all_to_all | solution.py:202
  12.5 83.1 %all-to-all-start = ((bf16[32,384,128]{2,1,0:T(8,128)(2,1)}), bf16[32,384,128]{2,1,0:T(8,128)(2,1)}, u32[]{:S(2)}, u32[]{:S(2)}) async-start(bf16[32,384,128]{2,1,0:T(8,128)(2,1)} %shard_map.91), calls=%async_computation | async-start | bytes 6291456 | tf_op jit(solution)/shard_map/all_to_all | solution.py:202
  24.2 80.0 %copy-start.7 = (f32[1,16]{1,0:T(1,128)S(1)}, f32[1,16]{1,0:T(1,128)}, u32[]{:S(2)}) copy-start(f32[1,16]{1,0:T(1,128)} %param.14) | copy-start | bytes 196
  24.2 80.3 %copy-start.8 = (s32[64]{0:T(128)S(1)}, s32[64]{0:T(128)}, u32[]{:S(2)}) copy-start(s32[64]{0:T(128)} %param.16) | copy-start | bytes 772
  24.2 80.8 %copy-start.4 = (s32[1,16]{1,0:T(1,128)S(1)}, s32[1,16]{1,0:T(1,128)}, u32[]{:S(2)}) copy-start(s32[1,16]{1,0:T(1,128)} %param.17) | copy-start | bytes 196
  95.7 38.6 %all-to-all-start.1 = ((bf16[32,128,128]{2,1,0:T(8,128)(2,1)}), bf16[32,128,128]{2,1,0:T(8,128)(2,1)S(1)}, u32[]{:S(2)}, u32[]{:S(2)}) async-start(bf16[32,128,128]{2,1,0:T(8,128)(2,1)} %shard_map.93), calls=%async_computation.1 | async-start | bytes 2097152 | tf_op jit(solution)/shard_map/all_to_all | solution.py:202
  104.6 28.1 %copy-start.3 = (s32[64]{0:T(128)}, s32[64]{0:T(128)S(1)}, u32[]{:S(2)}) copy-start(s32[64]{0:T(128)S(1)} %select_reduce_fusion.place) | copy-start | bytes 772
  132.7 1.0 copy-start.1
  133.7 0.6 copy-start.2
  134.3 1.0 copy-start.5
  137.8 11.0 %all-to-all-start.2 = ((f32[8,16,128]{2,1,0:T(8,128)}), f32[8,16,128]{2,1,0:T(8,128)S(1)}, u32[]{:S(2)}, u32[]{:S(2)}) async-start(f32[8,16,128]{2,1,0:T(8,128)} %shard_map.94), calls=%async_computation.2 | async-start | bytes 131072 | tf_op jit(solution)/shard_map/all_to_all | solution.py:202
  148.9 0.6 copy-start.6
where the time goes:
time: 152 us; the launch traced here: 151 us
  waiting for transfers between devices  75.2 us (49%)
  Pallas kernels  40.1 us (26%)
  starting transfers between devices  29.8 us (20%)
  local copies, waits for them, and re-layouts  4.69 us (3%)
    all_to_all x4, waiting for transfers between devices, exchange(): return lax.all_to_all(value, axis, split_axis=0, concat_axis=0, tiled=True)  75.2 us
    all_to_all x4, starting transfers between devices, exchange(): return lax.all_to_all(value, axis, split_axis=0, concat_axis=0, tiled=True)  29.8 us
    pallas_call x1, Pallas kernels, attend(): pl.pallas_call(functools.partial(attend_kernel, per_group=per_group, grou...  27.7 us
    pallas_call x2, Pallas kernels, to_panels(): pl.pallas_call(functools.partial(kernel, panel=panel), grid=(frames // st...  8.01 us
    unnamed x18, local copies, waits for them, and re-layouts  3.22 us
  transfers between devices with their start and end apart: 4, of which 3 were waited for; matrix products, arithmetic and copies ran while one was open for 1% of the time, Pallas kernels for 24%

commit v1 on v0

--- a/solution.py
+++ b/solution.py
@@ -8,7 +8,7 @@
 from jax.experimental.pallas import tpu as pltpu
 from jax.sharding import PartitionSpec as P
 
-HEAD_DIM = 128
+
 CHUNK = 4
 
 
@@ -144,31 +144,34 @@
     )(place, start, qkv, gate)
 
 
-def combine_kernel(place, attn, square, diff, out, *, per_group, groups):
-    block_len, dim = diff.shape[1], diff.shape[2]
-
-    for c in range(groups):
-        acc = jnp.zeros((8, dim), jnp.float32)
-        for b in range(per_group):
-            t = c * per_group + b
-            product = attn[t * block_len : (t + 1) * block_len, :].astype(jnp.float32) * diff[
-                place[t]
-            ].astype(jnp.float32)
-            acc = acc + jnp.sum(product.reshape(block_len // 8, 8, dim), axis=0)
-        row = jnp.sum(acc, axis=0, keepdims=True) + square[c : c + 1, :]
-        for copy in range(out.shape[0]):
-            out[copy, c : c + 1, :] = row
-
-
-def combine(place, attn, square, diff, copies, per_group, groups):
+def combine_kernel(when, attn, square, *refs, per_group):
+    parts, out, sums = refs[:-2], refs[-2], refs[-1]
+    block_len, _ = parts[0].shape[1:]
+    sums[...] = square[...]
+    at = 0
+    for part in parts:
+        for k in range(part.shape[0]):
+            t = when[at]
+            at += 1
+            rows = pl.ds(pl.multiple_of(t * block_len, block_len), block_len)
+            product = attn[rows, :].astype(jnp.float32) * part[k].astype(jnp.float32)
+            row = pl.ds(t // per_group, 1)
+            sums[row, :] = sums[row, :] + jnp.sum(product, axis=0, keepdims=True)
+    for copy in range(out.shape[0]):
+        out[copy] = sums[...]
+
+
+def combine(when, attn, square, parts, copies, per_group):
     smem = pl.BlockSpec(memory_space=pltpu.SMEM)
     vmem = pl.BlockSpec(memory_space=pltpu.VMEM)
     return pl.pallas_call(
-        functools.partial(combine_kernel, per_group=per_group, groups=groups),
-        in_specs=[smem, vmem, vmem, vmem],
+        functools.partial(combine_kernel, per_group=per_group),
+        in_specs=[smem, vmem, vmem] + [vmem] * len(parts),
         out_specs=vmem,
-        out_shape=jax.ShapeDtypeStruct((copies, groups, attn.shape[1]), jnp.float32),
-    )(place, attn, square, diff)
+        out_shape=jax.ShapeDtypeStruct((copies, *square.shape), jnp.float32),
+        scratch_shapes=[pltpu.VMEM(square.shape, jnp.float32)],
+        compiler_params=pltpu.CompilerParams(vmem_limit_bytes=16 * 1024 * 1024),
+    )(when, attn, square, *parts)
 
 
 def finish_kernel(sums, embed, out, *, root):
@@ -188,6 +191,7 @@
     return pl.pallas_call(
         functools.partial(finish_kernel, root=root),
         out_shape=jax.ShapeDtypeStruct((sums.shape[1], embed.shape[1]), jnp.float32),
+        compiler_params=pltpu.CompilerParams(vmem_limit_bytes=16 * 1024 * 1024),
     )(sums, embed)
 
 
@@ -200,6 +204,32 @@
 
 def exchange(value, axis):
     return lax.all_to_all(value, axis, split_axis=0, concat_axis=0, tiled=True)
+
+
+def swap(value, axis, mask):
+    pairs = [(i, i ^ mask) for i in range(lax.axis_size(axis))]
+    return lax.ppermute(value, axis, pairs)
+
+
+def exchange_by_swaps(panels, index):
+    near = (0, 1, 16, 17)
+    shape = panels.shape[1:]
+    cube = panels.reshape(2, 8, 2, *shape)
+    first = []
+    for mask in near:
+        sent = lax.dynamic_slice(
+            cube,
+            ((index >> 4) ^ (mask >> 4), 0, (index & 1) ^ (mask & 1)) + (0,) * len(shape),
+            (1, 8, 1, *shape),
+        ).reshape(8, *shape)
+        first.append(sent if mask == 0 else swap(sent, "frame", mask))
+    first = jnp.stack(first, axis=1)
+    parts = []
+    for z in range(8):
+        sent = lax.dynamic_index_in_dim(first, ((index >> 1) & 7) ^ z, 0, keepdims=False)
+        parts.append(sent if z == 0 else swap(sent, "frame", 2 * z))
+    masks = [m + 2 * z for z in range(8) for m in near]
+    return parts, masks
 
 
 def per_device(
@@ -216,7 +246,17 @@
     per_group = blocks // groups
     root = math.sqrt(per_group * block_len)
 
-    noise_all = exchange(jnp.broadcast_to(noise_level[None], (streams, 1, groups)), "stream")
+    stream = lax.axis_index("stream")
+    qkv = to_panels(panels_kernel, (query[0], key[0], value[0]), frames, 3)
+    qkv = exchange(qkv, "frame")
+    diff = to_panels(difference_kernel, (latent[0], target[0]), frames, 1)
+    parts, masks = exchange_by_swaps(diff, index)
+    noise = noise_level
+    for mask in (1, 2, 4):
+        noise = jnp.concatenate([noise, swap(noise, "stream", mask)])
+    owner = jnp.arange(streams, dtype=jnp.int32) ^ stream
+    pick = owner[None, :] == jnp.arange(streams, dtype=jnp.int32)[:, None]
+    noise_all = jnp.sum(jnp.where(pick[:, :, None], noise[None], 0.0), axis=1)
     embed_all = sinusoid(noise_all.reshape(streams * groups), mod_weight.shape[1])
     embed_own = sinusoid(noise_level[0], mod_weight.shape[1])
     weight_rows = lax.dynamic_slice_in_dim(mod_weight, index * local_width, local_width, 0)
@@ -225,21 +265,15 @@
     )
     times = jnp.arange(blocks, dtype=jnp.int32)
     place = jnp.sum(jnp.where(block_order[None, :] == times[:, None], times[None, :], 0), axis=1)
-
-    qkv = to_panels(panels_kernel, (query[0], key[0], value[0]), frames, 3)
-    diff = to_panels(difference_kernel, (latent[0], target[0]), frames, 1)
-    qkv = exchange(qkv, "frame")
-    diff = exchange(diff, "frame")
+    slots = jnp.array([2 * m + b for m in masks for b in range(2)], jnp.int32) ^ (2 * index)
+    when = jnp.sum(jnp.where(slots[:, None] == times[None, :], block_order[None, :], 0), axis=1)
     attn, square = attend(
         place, context_start[0], qkv.reshape(frames * 6, block_len, local_width), gate, per_group, groups
     )
-    sums = combine(
-        place, attn, square, diff.reshape(frames * 2, block_len, local_width), streams, per_group, groups
-    )
+    parts = [p.reshape(-1, block_len, local_width) for p in parts]
+    sums = combine(when, attn, square, parts, streams, per_group)
     sums = exchange(sums, "stream")
-    return finish(
-        sums.reshape(streams * groups, local_width), embed_all.astype(jnp.float32), root
-    )
+    return finish(sums.reshape(streams * groups, local_width), embed_all.astype(jnp.float32), root)
 
 
 def solution(mesh):

time: 152 us -> 146 us (0.961)
  the two profiles are of different devices: /device:TPU:16 before, /device:TPU:48 now
where the time goes in v1:
time: 146 us
  waiting for transfers between devices  60.9 us (42%)
  starting transfers between devices  41.9 us (29%)
  Pallas kernels  38.4 us (26%)
  local copies, waits for them, and re-layouts  2.2 us (2%)
  other arithmetic  1.93 us (1%)
    ppermute x13, waiting for transfers between devices, swap(): return lax.ppermute(value, axis, pairs)  54.6 us
    pallas_call x1, Pallas kernels, attend(): pl.pallas_call(functools.partial(attend_kernel, per_group=per_group, grou...  27.7 us
    ppermute x13, starting transfers between devices, swap(): return lax.ppermute(value, axis, pairs)  25.1 us
    all_to_all x2, starting transfers between devices, exchange(): return lax.all_to_all(value, axis, split_axis=0, concat_axis=0, tiled=True)  16.8 us
    pallas_call x2, Pallas kernels, to_panels(): pl.pallas_call(functools.partial(kernel, panel=panel), grid=(frames // st...  8.15 us
    all_to_all x2, waiting for transfers between devices, exchange(): return lax.all_to_all(value, axis, split_axis=0, concat_axis=0, tiled=True)  6.34 us
  transfers between devices with their start and end apart: 15, of which 7 were waited for; matrix products, arithmetic and copies ran while one was open for 3% of the time, Pallas kernels for 22%

profile of v1, /device:TPU:48, one launch (start us, length us, event | category | flops | bytes accessed | tf_op | source)
XLA Modules:
  0.0 145.6 jit_solution(12507108282881004341)
XLA Ops:
  0.0 0.0 copy-start
  0.0 4.5 %shard_map.100 = bf16[32,384,128]{2,1,0:T(8,128)(2,1)} custom-call(bf16[128,4096]{1,0:T(8,128)(2,1)} %bitcast.57, bf16[128,4096]{1,0:T(8,128)(2,1)} %bitcast.58, bf16[128,4096]{1,0:T(8,128)(2,1)} %bitcast.59), custom_call_target="tpu_custom_call" | custom-call | tf_op jit(solution)/shard_map/pallas_call | solution.py:34
  4.5 11.2 %all-to-all-start = ((bf16[32,384,128]{2,1,0:T(8,128)(2,1)}), bf16[32,384,128]{2,1,0:T(8,128)(2,1)}, u32[]{:S(2)}, u32[]{:S(2)}) async-start(bf16[32,384,128]{2,1,0:T(8,128)(2,1)} %shard_map.100), calls=%async_computation | async-start | bytes 6291456 | tf_op jit(solution)/shard_map/all_to_all | solution.py:206
  15.7 0.0 copy-start.2
  15.7 0.0 copy-start.4
  15.8 0.0 copy-start.3
  15.8 3.6 %shard_map.102 = bf16[32,128,128]{2,1,0:T(8,128)(2,1)} custom-call(bf16[128,4096]{1,0:T(8,128)(2,1)} %bitcast.55, bf16[128,4096]{1,0:T(8,128)(2,1)} %bitcast.56), custom_call_target="tpu_custom_call" | custom-call | tf_op jit(solution)/shard_map/pallas_call | solution.py:34
  19.4 1.3 dynamic-slice_bitcast_fusion.3
  20.7 0.4 collective-permute-start.2
  21.1 3.0 %collective-permute-start.1 = (bf16[8,128,128]{2,1,0:T(8,128)(2,1)S(1)}, bf16[8,128,128]{2,1,0:T(8,128)(2,1)}, u32[]{:S(2)}, u32[]{:S(2)}) collective-permute-start(bf16[8,128,128]{2,1,0:T(8,128)(2,1)S(1)} %get-tuple-element.21), channel_id=1, source_target_pairs={{0,128},{8,136},{16,144},{24,152},{32,160},{40,168},{48,176},{56,1... | collective-permute-start | bytes 786440 | tf_op jit(solution)/shard_map/ppermute | solution.py:211
  24.0 0.1 collective-permute-start
  24.2 0.0 copy-done.2
  24.2 1.5 %collective-permute-start.10 = (f32[1,16]{1,0:T(1,128)S(1)}, f32[1,16]{1,0:T(1,128)S(1)}, u32[]{:S(2)}, u32[]{:S(2)}) collective-permute-start(f32[1,16]{1,0:T(1,128)S(1)} %copy-done.2), channel_id=1, source_target_pairs={{0,1},{1,0},{2,3},{3,2},{4,5},{5,4},{6,7},{7,6},{8,9},{9,8},{10,11... | collective-permute-start | bytes 200 | tf_op jit(solution)/shard_map/ppermute | solution.py:211
  25.7 0.1 fusion.4
  25.8 0.0 copy-done
  25.8 0.1 fusion.2.gate
  25.9 0.0 copy-done.4
  25.9 0.0 copy-done.3
  26.0 0.2 select_reduce_fusion.1
  26.2 1.6 %collective-permute-done.10 = f32[1,16]{1,0:T(1,128)S(1)} collective-permute-done((f32[1,16]{1,0:T(1,128)S(1)}, f32[1,16]{1,0:T(1,128)S(1)}, u32[]{:S(2)}, u32[]{:S(2)}) %collective-permute-start.10) | collective-permute-done | bytes 96 | tf_op jit(solution)/shard_map/ppermute | solution.py:211
  27.7 3.1 %collective-permute-start.11 = (f32[2,16]{1,0:T(2,128)S(1)}, f32[2,16]{1,0:T(2,128)S(1)}, u32[]{:S(2)}, u32[]{:S(2)}) collective-permute-start(f32[2,16]{1,0:T(2,128)S(1)} %pad_maximum_fusion.3), channel_id=1, source_target_pairs={{0,2},{1,3},{2,0},{3,1},{4,6},{5,7},{6,4},{7,5},{8,10},{9,11},{10,... | collective-permute-start | bytes 392 | tf_op jit(solution)/shard_map/ppermute | solution.py:211
  30.8 2.1 %collective-permute-done.11 = f32[2,16]{1,0:T(2,128)S(1)} collective-permute-done((f32[2,16]{1,0:T(2,128)S(1)}, f32[2,16]{1,0:T(2,128)S(1)}, u32[]{:S(2)}, u32[]{:S(2)}) %collective-permute-start.11) | collective-permute-done | bytes 160 | tf_op jit(solution)/shard_map/ppermute | solution.py:211
  32.9 1.4 collective-permute-start.12
  34.3 7.2 %collective-permute-done.12 = f32[4,16]{1,0:T(4,128)S(1)} collective-permute-done((f32[4,16]{1,0:T(4,128)S(1)}, f32[4,16]{1,0:T(4,128)S(1)}, u32[]{:S(2)}, u32[]{:S(2)}) %collective-permute-start.12) | collective-permute-done | bytes 288 | tf_op jit(solution)/shard_map/ppermute | solution.py:211
  41.5 0.1 select_reduce_fusion
  41.6 0.1 mul.69
  41.6 0.0 collective-permute-done.2
  41.6 8.3 %collective-permute-done.1 = bf16[8,128,128]{2,1,0:T(8,128)(2,1)} collective-permute-done((bf16[8,128,128]{2,1,0:T(8,128)(2,1)S(1)}, bf16[8,128,128]{2,1,0:T(8,128)(2,1)}, u32[]{:S(2)}, u32[]{:S(2)}) %collective-permute-start.1) | collective-permute-done | bytes 262176 | tf_op jit(solution)/shard_map/ppermute | solution.py:211
  49.9 0.0 collective-permute-done
  49.9 0.0 copy-start.1
  49.9 1.2 pad_maximum_fusion
  51.1 0.8 dynamic-slice_bitcast_fusion.4
  51.9 0.0 collective-permute-start.3
  51.9 0.0 collective-permute-start.4
  51.9 0.3 fusion
  52.2 3.6 %collective-permute-start.5 = (bf16[4,128,128]{2,1,0:T(8,128)(2,1)}, bf16[4,128,128]{2,1,0:T(8,128)(2,1)S(1)}, u32[]{:S(2)}, u32[]{:S(2)}) collective-permute-start(bf16[4,128,128]{2,1,0:T(8,128)(2,1)} %get-tuple-element.15), channel_id=1, source_target_pairs={{0,48},{8,56},{16,32},{24,40},{32,16},{40,24},{48,0},{56,8},{64,11... | collective-permute-start | bytes 393224 | tf_op jit(solution)/shard_map/ppermute | solution.py:211
  55.8 3.3 %collective-permute-start.6 = (bf16[4,128,128]{2,1,0:T(8,128)(2,1)}, bf16[4,128,128]{2,1,0:T(8,128)(2,1)S(1)}, u32[]{:S(2)}, u32[]{:S(2)}) collective-permute-start(bf16[4,128,128]{2,1,0:T(8,128)(2,1)} %get-tuple-element.14), channel_id=1, source_target_pairs={{0,64},{8,72},{16,80},{24,88},{32,96},{40,104},{48,112},{56,120},{... | collective-permute-start | bytes 393224 | tf_op jit(solution)/shard_map/ppermute | solution.py:211
  59.1 2.1 %collective-permute-start.7 = (bf16[4,128,128]{2,1,0:T(8,128)(2,1)}, bf16[4,128,128]{2,1,0:T(8,128)(2,1)S(1)}, u32[]{:S(2)}, u32[]{:S(2)}) collective-permute-start(bf16[4,128,128]{2,1,0:T(8,128)(2,1)} %get-tuple-element.13), channel_id=1, source_target_pairs={{0,80},{8,88},{16,64},{24,72},{32,112},{40,120},{48,96},{56,104},{... | collective-permute-start | bytes 393224 | tf_op jit(solution)/shard_map/ppermute | solution.py:211
  61.1 31.6 %collective-permute-done.3 = bf16[4,128,128]{2,1,0:T(8,128)(2,1)S(1)} collective-permute-done((bf16[4,128,128]{2,1,0:T(8,128)(2,1)S(1)}, bf16[4,128,128]{2,1,0:T(8,128)(2,1)S(1)}, u32[]{:S(2)}, u32[]{:S(2)}) %collective-permute-start.3) | collective-permute-done | bytes 131104 | tf_op jit(solution)/shard_map/ppermute | solution.py:211
  92.7 1.7 %collective-permute-start.8 = (bf16[4,128,128]{2,1,0:T(8,128)(2,1)S(1)}, bf16[4,128,128]{2,1,0:T(8,128)(2,1)S(1)}, u32[]{:S(2)}, u32[]{:S(2)}) collective-permute-start(bf16[4,128,128]{2,1,0:T(8,128)(2,1)S(1)} %get-tuple-element.12), channel_id=1, source_target_pairs={{0,96},{8,104},{16,112},{24,120},{32,64},{40,72},{48,80},{56,88},{... | collective-permute-start | bytes 393224 | tf_op jit(solution)/shard_map/ppermute | solution.py:211
  94.5 4.0 %collective-permute-done.4 = bf16[4,128,128]{2,1,0:T(8,128)(2,1)S(1)} collective-permute-done((bf16[4,128,128]{2,1,0:T(8,128)(2,1)S(1)}, bf16[4,128,128]{2,1,0:T(8,128)(2,1)S(1)}, u32[]{:S(2)}, u32[]{:S(2)}) %collective-permute-start.4) | collective-permute-done | bytes 131104 | tf_op jit(solution)/shard_map/ppermute | solution.py:211
  98.4 5.0 %collective-permute-start.9 = (bf16[4,128,128]{2,1,0:T(8,128)(2,1)S(1)}, bf16[4,128,128]{2,1,0:T(8,128)(2,1)S(1)}, u32[]{:S(2)}, u32[]{:S(2)}) collective-permute-start(bf16[4,128,128]{2,1,0:T(8,128)(2,1)S(1)} %get-tuple-element.11), channel_id=1, source_target_pairs={{0,112},{8,120},{16,96},{24,104},{32,80},{40,88},{48,64},{56,72},{... | collective-permute-start | bytes 393224 | tf_op jit(solution)/shard_map/ppermute | solution.py:211
  103.4 0.0 all-to-all-done
  103.4 0.0 copy-done.1
  103.4 27.7 %shard_map.101 = (bf16[4096,128]{1,0:T(8,128)(2,1)S(1)}, f32[16,128]{1,0:T(8,128)S(1)}) custom-call(s32[64]{0:T(128)S(1)} %get-tuple-element.9.place, s32[16]{0:T(128)S(1)} %bitcast.53, bf16[192,64,128]{2,1,0:T(8,128)(2,1)} %bitcast.4.qkv, f32[16,128]{1,0:T(8,128)S(1)} %fusion.2.gate), custom_call_target="tpu_custom_call" | custom-call | flops 8589934592 | bytes 4194304 | tf_op jit(solution)/shard_map/pallas_call | solution.py:126
  131.1 0.0 collective-permute-done.5
  131.1 0.0 collective-permute-done.6
  131.1 0.0 collective-permute-done.7
  131.2 0.0 collective-permute-done.8
  131.2 0.0 collective-permute-done.9
  131.2 1.6 %shard_map.103 = f32[8,16,128]{2,1,0:T(8,128)} custom-call(s32[64]{0:T(128)S(1)} %get-tuple-element.10.when, bf16[4096,128]{1,0:T(8,128)(2,1)S(1)} %get-tuple-element.7.attn, f32[16,128]{1,0:T(8,128)S(1)} %get-tuple-element.8.square, bf16[8,64,128]{2,1,0:T(8,128)(2,1)S(1)} %bitcast.44, bf16[8,64,128]{2,1,0:T(8,128)(2,1)S(1)} %bitcast.46, ...), custom_call_target="tpu_custom_call" | custom-call | tf_op jit(solution)/shard_map/pallas_call | solution.py:167
  132.7 5.6 %all-to-all-start.1 = ((f32[8,16,128]{2,1,0:T(8,128)}), f32[8,16,128]{2,1,0:T(8,128)S(1)}, u32[]{:S(2)}, u32[]{:S(2)}) async-start(f32[8,16,128]{2,1,0:T(8,128)} %shard_map.103), calls=%async_computation.1 | async-start | bytes 131072 | tf_op jit(solution)/shard_map/all_to_all | solution.py:206
  138.3 6.3 %all-to-all-done.1 = f32[8,16,128]{2,1,0:T(8,128)S(1)} async-done(((f32[8,16,128]{2,1,0:T(8,128)}), f32[8,16,128]{2,1,0:T(8,128)S(1)}, u32[]{:S(2)}, u32[]{:S(2)}) %all-to-all-start.1) | async-done | bytes 65568 | tf_op jit(solution)/shard_map/all_to_all | solution.py:206
  144.7 1.0 shard_map.104
  (10 shorter events, 0.1 us)
Async XLA Ops:
  0.0 25.8 %copy-start = (bf16[4096,256]{1,0:T(8,128)(2,1)S(1)}, bf16[4096,256]{1,0:T(8,128)(2,1)}, u32[]{:S(2)}) copy-start(bf16[4096,256]{1,0:T(8,128)(2,1)} %param.16) | copy-start | bytes 6291460
  4.5 98.9 %all-to-all-start = ((bf16[32,384,128]{2,1,0:T(8,128)(2,1)}), bf16[32,384,128]{2,1,0:T(8,128)(2,1)}, u32[]{:S(2)}, u32[]{:S(2)}) async-start(bf16[32,384,128]{2,1,0:T(8,128)(2,1)} %shard_map.100), calls=%async_computation | async-start | bytes 6291456 | tf_op jit(solution)/shard_map/all_to_all | solution.py:206
  15.7 8.4 %copy-start.2 = (f32[1,16]{1,0:T(1,128)S(1)}, f32[1,16]{1,0:T(1,128)}, u32[]{:S(2)}) copy-start(f32[1,16]{1,0:T(1,128)} %param.15) | copy-start | bytes 196
  15.7 10.2 %copy-start.4 = (s32[64]{0:T(128)S(1)}, s32[64]{0:T(128)}, u32[]{:S(2)}) copy-start(s32[64]{0:T(128)} %constant.60.clone) | copy-start | bytes 772
  15.8 10.2 %copy-start.3 = (s32[64]{0:T(128)S(1)}, s32[64]{0:T(128)}, u32[]{:S(2)}) copy-start(s32[64]{0:T(128)} %param.17) | copy-start | bytes 772
  20.7 20.9 %collective-permute-start.2 = (bf16[8,128,128]{2,1,0:T(8,128)(2,1)S(1)}, bf16[8,128,128]{2,1,0:T(8,128)(2,1)S(1)}, u32[]{:S(2)}, u32[]{:S(2)}) collective-permute-start(bf16[8,128,128]{2,1,0:T(8,128)(2,1)S(1)} %get-tuple-element.20), channel_id=1, source_target_pairs={{0,136},{8,128},{16,152},{24,144},{32,168},{40,160},{48,184},{56,1... | collective-permute-start | bytes 786440 | tf_op jit(solution)/shard_map/ppermute | solution.py:211
  21.1 28.8 %collective-permute-start.1 = (bf16[8,128,128]{2,1,0:T(8,128)(2,1)S(1)}, bf16[8,128,128]{2,1,0:T(8,128)(2,1)}, u32[]{:S(2)}, u32[]{:S(2)}) collective-permute-start(bf16[8,128,128]{2,1,0:T(8,128)(2,1)S(1)} %get-tuple-element.21), channel_id=1, source_target_pairs={{0,128},{8,136},{16,144},{24,152},{32,160},{40,168},{48,176},{56,1... | collective-permute-start | bytes 786440 | tf_op jit(solution)/shard_map/ppermute | solution.py:211
  24.0 25.9 %collective-permute-start = (bf16[8,128,128]{2,1,0:T(8,128)(2,1)S(1)}, bf16[8,128,128]{2,1,0:T(8,128)(2,1)}, u32[]{:S(2)}, u32[]{:S(2)}) collective-permute-start(bf16[8,128,128]{2,1,0:T(8,128)(2,1)S(1)} %get-tuple-element.22), channel_id=1, source_target_pairs={{0,8},{8,0},{16,24},{24,16},{32,40},{40,32},{48,56},{56,48},{64,72... | collective-permute-start | bytes 786440 | tf_op jit(solution)/shard_map/ppermute | solution.py:211
  24.2 3.6 %collective-permute-start.10 = (f32[1,16]{1,0:T(1,128)S(1)}, f32[1,16]{1,0:T(1,128)S(1)}, u32[]{:S(2)}, u32[]{:S(2)}) collective-permute-start(f32[1,16]{1,0:T(1,128)S(1)} %copy-done.2), channel_id=1, source_target_pairs={{0,1},{1,0},{2,3},{3,2},{4,5},{5,4},{6,7},{7,6},{8,9},{9,8},{10,11... | collective-permute-start | bytes 200 | tf_op jit(solution)/shard_map/ppermute | solution.py:211
  27.7 5.2 %collective-permute-start.11 = (f32[2,16]{1,0:T(2,128)S(1)}, f32[2,16]{1,0:T(2,128)S(1)}, u32[]{:S(2)}, u32[]{:S(2)}) collective-permute-start(f32[2,16]{1,0:T(2,128)S(1)} %pad_maximum_fusion.3), channel_id=1, source_target_pairs={{0,2},{1,3},{2,0},{3,1},{4,6},{5,7},{6,4},{7,5},{8,10},{9,11},{10,... | collective-permute-start | bytes 392 | tf_op jit(solution)/shard_map/ppermute | solution.py:211
  32.9 8.5 %collective-permute-start.12 = (f32[4,16]{1,0:T(4,128)S(1)}, f32[4,16]{1,0:T(4,128)S(1)}, u32[]{:S(2)}, u32[]{:S(2)}) collective-permute-start(f32[4,16]{1,0:T(4,128)S(1)} %pad_maximum_fusion.2), channel_id=1, source_target_pairs={{0,4},{1,5},{2,6},{3,7},{4,0},{5,1},{6,2},{7,3},{8,12},{9,13},{10,... | collective-permute-start | bytes 776 | tf_op jit(solution)/shard_map/ppermute | solution.py:211
  49.9 53.5 %copy-start.1 = (s32[1,16]{1,0:T(1,128)S(1)}, s32[1,16]{1,0:T(1,128)}, u32[]{:S(2)}) copy-start(s32[1,16]{1,0:T(1,128)} %param.18) | copy-start | bytes 196
  51.9 40.8 %collective-permute-start.3 = (bf16[4,128,128]{2,1,0:T(8,128)(2,1)S(1)}, bf16[4,128,128]{2,1,0:T(8,128)(2,1)S(1)}, u32[]{:S(2)}, u32[]{:S(2)}) collective-permute-start(bf16[4,128,128]{2,1,0:T(8,128)(2,1)S(1)} %get-tuple-element.17), channel_id=1, source_target_pairs={{0,16},{8,24},{16,0},{24,8},{32,48},{40,56},{48,32},{56,40},{64,80... | collective-permute-start | bytes 393224 | tf_op jit(solution)/shard_map/ppermute | solution.py:211
  51.9 46.5 %collective-permute-start.4 = (bf16[4,128,128]{2,1,0:T(8,128)(2,1)S(1)}, bf16[4,128,128]{2,1,0:T(8,128)(2,1)S(1)}, u32[]{:S(2)}, u32[]{:S(2)}) collective-permute-start(bf16[4,128,128]{2,1,0:T(8,128)(2,1)S(1)} %get-tuple-element.16), channel_id=1, source_target_pairs={{0,32},{8,40},{16,48},{24,56},{32,0},{40,8},{48,16},{56,24},{64,96... | collective-permute-start | bytes 393224 | tf_op jit(solution)/shard_map/ppermute | solution.py:211
  52.2 78.9 %collective-permute-start.5 = (bf16[4,128,128]{2,1,0:T(8,128)(2,1)}, bf16[4,128,128]{2,1,0:T(8,128)(2,1)S(1)}, u32[]{:S(2)}, u32[]{:S(2)}) collective-permute-start(bf16[4,128,128]{2,1,0:T(8,128)(2,1)} %get-tuple-element.15), channel_id=1, source_target_pairs={{0,48},{8,56},{16,32},{24,40},{32,16},{40,24},{48,0},{56,8},{64,11... | collective-permute-start | bytes 393224 | tf_op jit(solution)/shard_map/ppermute | solution.py:211
  55.8 75.4 %collective-permute-start.6 = (bf16[4,128,128]{2,1,0:T(8,128)(2,1)}, bf16[4,128,128]{2,1,0:T(8,128)(2,1)S(1)}, u32[]{:S(2)}, u32[]{:S(2)}) collective-permute-start(bf16[4,128,128]{2,1,0:T(8,128)(2,1)} %get-tuple-element.14), channel_id=1, source_target_pairs={{0,64},{8,72},{16,80},{24,88},{32,96},{40,104},{48,112},{56,120},{... | collective-permute-start | bytes 393224 | tf_op jit(solution)/shard_map/ppermute | solution.py:211
  59.1 72.1 %collective-permute-start.7 = (bf16[4,128,128]{2,1,0:T(8,128)(2,1)}, bf16[4,128,128]{2,1,0:T(8,128)(2,1)S(1)}, u32[]{:S(2)}, u32[]{:S(2)}) collective-permute-start(bf16[4,128,128]{2,1,0:T(8,128)(2,1)} %get-tuple-element.13), channel_id=1, source_target_pairs={{0,80},{8,88},{16,64},{24,72},{32,112},{40,120},{48,96},{56,104},{... | collective-permute-start | bytes 393224 | tf_op jit(solution)/shard_map/ppermute | solution.py:211
  92.7 38.4 %collective-permute-start.8 = (bf16[4,128,128]{2,1,0:T(8,128)(2,1)S(1)}, bf16[4,128,128]{2,1,0:T(8,128)(2,1)S(1)}, u32[]{:S(2)}, u32[]{:S(2)}) collective-permute-start(bf16[4,128,128]{2,1,0:T(8,128)(2,1)S(1)} %get-tuple-element.12), channel_id=1, source_target_pairs={{0,96},{8,104},{16,112},{24,120},{32,64},{40,72},{48,80},{56,88},{... | collective-permute-start | bytes 393224 | tf_op jit(solution)/shard_map/ppermute | solution.py:211
  98.4 32.7 %collective-permute-start.9 = (bf16[4,128,128]{2,1,0:T(8,128)(2,1)S(1)}, bf16[4,128,128]{2,1,0:T(8,128)(2,1)S(1)}, u32[]{:S(2)}, u32[]{:S(2)}) collective-permute-start(bf16[4,128,128]{2,1,0:T(8,128)(2,1)S(1)} %get-tuple-element.11), channel_id=1, source_target_pairs={{0,112},{8,120},{16,96},{24,104},{32,80},{40,88},{48,64},{56,72},{... | collective-permute-start | bytes 393224 | tf_op jit(solution)/shard_map/ppermute | solution.py:211
  132.7 11.9 %all-to-all-start.1 = ((f32[8,16,128]{2,1,0:T(8,128)}), f32[8,16,128]{2,1,0:T(8,128)S(1)}, u32[]{:S(2)}, u32[]{:S(2)}) async-start(f32[8,16,128]{2,1,0:T(8,128)} %shard_map.103), calls=%async_computation.1 | async-start | bytes 131072 | tf_op jit(solution)/shard_map/all_to_all | solution.py:206

commit v2 on v1

--- a/solution.py
+++ b/solution.py
@@ -10,6 +10,7 @@
 
 
 CHUNK = 4
+ROWS = 32
 
 
 def panels_kernel(*refs, panel):
@@ -27,127 +28,202 @@
         out[k] = wide.astype(jnp.bfloat16)
 
 
-def to_panels(kernel, arrays, frames, stacked):
+def to_panels(kernel, arrays, frames, stacked, limit=None, steps=2):
     rows, width = arrays[0].shape
     panel = width // frames
-    step = max(1, frames // 4)
+    step = max(1, frames // steps)
     return pl.pallas_call(
         functools.partial(kernel, panel=panel),
         grid=(frames // step,),
         in_specs=[pl.BlockSpec((rows, step * panel), lambda i: (0, i))] * len(arrays),
         out_specs=pl.BlockSpec((step, stacked * rows, panel), lambda i: (i, 0, 0)),
         out_shape=jax.ShapeDtypeStruct((frames, stacked * rows, panel), jnp.bfloat16),
+        compiler_params=pltpu.CompilerParams(vmem_limit_bytes=limit),
     )(*arrays)
 
 
 def attend_kernel(
-    place, start, qkv, gate, attn_out, square_out, q_sorted, k_sorted, v_sorted, strip, *, per_group, groups
+    order,
+    start,
+    qkv,
+    gate,
+    attn_out,
+    square_out,
+    landing,
+    q_sorted,
+    k_sorted,
+    v_sorted,
+    strip,
+    levels,
+    tops,
+    totals,
+    group_of,
+    tile_of,
+    sems,
+    *,
+    per_group,
+    groups,
 ):
     block_len, dim = qkv.shape[1], qkv.shape[2]
     blocks = per_group * groups
     rows = per_group * block_len
-    scale = 1.0 / math.sqrt(dim)
-
-    def sort_block(t, carry):
-        p = place[t]
-        base = (p // 2) * 6 + p % 2
-        at = pl.ds(pl.multiple_of(t * block_len, block_len), block_len)
-        q_sorted[at, :] = qkv[base]
-        k_sorted[at, :] = qkv[base + 2]
-        v_sorted[at, :] = qkv[base + 4]
-        return carry
-
-    lax.fori_loop(0, blocks, sort_block, 0, unroll=8)
+    wide = CHUNK * rows
+    factor = math.log2(math.e) / math.sqrt(dim)
+    pieces = sems.shape[0]
+    piece = qkv.shape[0] // pieces
+
+    def fetch(n):
+        part = pl.ds(n * piece, piece)
+        return pltpu.make_async_copy(qkv.at[part], landing.at[part], sems.at[n])
+
+    for n in range(pieces):
+        fetch(n).start()
+
+    def list_group(c, at):
+        def list_chunk(j, at):
+            group_of[at] = c
+            tile_of[at] = start[c] + j * CHUNK
+            return at + 1
+
+        return lax.fori_loop(0, (c - start[c] + CHUNK) // CHUNK, list_chunk, at)
+
+    chunks = lax.fori_loop(0, groups, list_group, 0)
+
     pad = jnp.zeros(((CHUNK - 1) * rows, dim), jnp.bfloat16)
     k_sorted[blocks * block_len :, :] = pad
     v_sorted[blocks * block_len :, :] = pad
-
-    def one_group(c, carry):
-        first = start[c]
-        count = c - first + 1
-        chunks = (count + CHUNK - 1) // CHUNK
-        at_q = pl.ds(pl.multiple_of(c * rows, rows), rows)
-        q = q_sorted[at_q, :]
-
-        def scores(i, peak):
+    levels[...] = jnp.zeros(levels.shape, jnp.float32)
+    per_piece = blocks // pieces
+    for n in range(pieces):
+        fetch(n).wait()
+
+        def sort_block(p, carry):
+            base = (p // 2) * 6 + p % 2
+            at = pl.ds(pl.multiple_of(order[p] * block_len, block_len), block_len)
+            q_sorted[at, :] = landing[base]
+            k_sorted[at, :] = landing[base + 2]
+            v_sorted[at, :] = landing[base + 4]
+            return carry
+
+        lax.fori_loop(n * per_piece, (n + 1) * per_piece, sort_block, 0, unroll=8)
+
+    def rows_of(ref, tile, count):
+        return ref[pl.ds(pl.multiple_of(tile * rows, rows), count), :]
+
+    def scores(t):
+        c, tile = group_of[t], tile_of[t]
+        s = lax.dot_general(
+            rows_of(q_sorted, c, rows),
+            rows_of(k_sorted, tile, wide),
+            (((1,), (1,)), ((), ())),
+            preferred_element_type=jnp.float32,
+        )
+        strip[t] = s
+
+    def normalize(t):
+        c, tile = group_of[t], tile_of[t]
+        fresh = tile == start[c]
+        for r in range(0, rows, ROWS):
+            at_r = slice(r, r + ROWS)
+            peak = None
             for u in range(CHUNK):
-                g = first + i * CHUNK + u
-                k = k_sorted[pl.ds(pl.multiple_of(g * rows, rows), rows), :]
-                s = lax.dot_general(
-                    q, k, (((1,), (1,)), ((), ())), preferred_element_type=jnp.float32
-                )
-                s = jnp.where(g <= c, s * scale, -jnp.inf)
-                strip[i * CHUNK + u] = s
+                top = strip[t, at_r, u * rows : u * rows + 128]
+                for b in range(1, rows // 128):
+                    top = jnp.maximum(top, strip[t, at_r, u * rows + b * 128 : u * rows + (b + 1) * 128])
+                peak = top if u == 0 else jnp.maximum(peak, jnp.where(tile + u <= c, top, -jnp.inf))
+            peak = jnp.broadcast_to(jnp.max(peak, axis=1, keepdims=True) * factor, (ROWS, 128))
+            before = jnp.where(fresh, -jnp.inf, tops[at_r, :])
+            top = jnp.maximum(before, peak)
+            total = totals[at_r, :] * jnp.exp2(before - top)
+            for u in range(CHUNK):
+                here = jnp.where(tile + u <= c, top, jnp.inf)
                 for b in range(rows // 128):
-                    peak = jnp.maximum(peak, s[:, b * 128 : (b + 1) * 128])
-            return peak
-
-        peak = lax.fori_loop(0, chunks, scores, jnp.full((rows, 128), -jnp.inf, jnp.float32))
-        peak = jnp.max(peak, axis=1, keepdims=True)
-
-        def exponents(i, total):
-            for u in range(CHUNK):
-                e = jnp.exp(strip[i * CHUNK + u] - peak)
-                strip[i * CHUNK + u] = e
-                for b in range(rows // 128):
-                    total = total + e[:, b * 128 : (b + 1) * 128]
-            return total
-
-        total = lax.fori_loop(0, chunks, exponents, jnp.zeros((rows, 128), jnp.float32))
-        inverse = 1.0 / jnp.sum(total, axis=1, keepdims=True)
-
-        def weigh(i, acc):
-            for u in range(CHUNK):
-                g = first + i * CHUNK + u
-                v = v_sorted[pl.ds(pl.multiple_of(g * rows, rows), rows), :]
-                probs = (strip[i * CHUNK + u] * inverse).astype(jnp.bfloat16)
-                acc = acc + lax.dot_general(
-                    probs, v, (((1,), (0,)), ((), ())), preferred_element_type=jnp.float32
-                )
-            return acc
-
-        acc = lax.fori_loop(0, chunks, weigh, jnp.zeros((rows, dim), jnp.float32))
+                    at = u * rows + b * 128
+                    total = total + jnp.exp2(strip[t, at_r, at : at + 128] * factor - here)
+            tops[at_r, :] = top
+            totals[at_r, :] = total
+            level = top + jnp.log2(jnp.sum(total, axis=1, keepdims=True))
+            lanes = lax.broadcasted_iota(jnp.int32, (ROWS, 128), 1)
+            levels[at_r, :] = jnp.where(lanes == c, level, levels[at_r, :])
+
+    def first_pass(t, carry):
+        normalize(t - 1)
+        scores(t)
+        return carry
+
+    totals[...] = jnp.zeros(totals.shape, jnp.float32)
+    tops[...] = jnp.zeros(tops.shape, jnp.float32)
+    scores(0)
+    lax.fori_loop(1, chunks, first_pass, 0)
+    normalize(chunks - 1)
+
+    def level_of(c):
+        lanes = lax.broadcasted_iota(jnp.int32, levels.shape, 1)
+        level = jnp.sum(jnp.where(lanes == c, levels[...], 0.0), axis=1, keepdims=True)
+        return jnp.broadcast_to(level, (rows, 128))
+
+    def second_pass(t, carry):
+        acc, level = carry
+        c, tile = group_of[t], tile_of[t]
+        probs = []
+        for u in range(CHUNK):
+            here = jnp.where(tile + u <= c, level, jnp.inf)
+            for b in range(rows // 128):
+                at = u * rows + b * 128
+                probs.append(jnp.exp2(strip[t, :, at : at + 128] * factor - here).astype(jnp.bfloat16))
+        part = lax.dot_general(
+            jnp.concatenate(probs, axis=1),
+            rows_of(v_sorted, tile, wide),
+            (((1,), (0,)), ((), ())),
+            preferred_element_type=jnp.float32,
+        )
+        level = level_of(group_of[jnp.minimum(t + 1, chunks - 1)])
+        acc = jnp.where(tile == start[c], 0.0, acc) + part
         rounded = acc.astype(jnp.bfloat16)
-        attn_out[at_q, :] = rounded
-        wide = rounded.astype(jnp.float32)
-        square_out[pl.ds(c, 1), :] = gate[pl.ds(c, 1), :] * jnp.sum(wide * wide, axis=0, keepdims=True)
-        return carry
-
-    lax.fori_loop(0, groups, one_group, 0)
-
-
-def attend(place, start, qkv, gate, per_group, groups):
+        attn_out[pl.ds(pl.multiple_of(c * rows, rows), rows), :] = rounded
+        back = rounded.astype(jnp.float32)
+        square_out[pl.ds(c, 1), :] = gate[pl.ds(c, 1), :] * jnp.sum(back * back, axis=0, keepdims=True)
+        return acc, level
+
+    lax.fori_loop(0, chunks, second_pass, (jnp.zeros((rows, dim), jnp.float32), level_of(0)))
+
+
+def attend(order, start, qkv, gate, per_group, groups):
     block_len, dim = qkv.shape[1], qkv.shape[2]
     length = per_group * groups * block_len
     rows = per_group * block_len
     smem = pl.BlockSpec(memory_space=pltpu.SMEM)
     vmem = pl.BlockSpec(memory_space=pltpu.VMEM)
     padded = length + (CHUNK - 1) * rows
+    most = sum((c + CHUNK) // CHUNK for c in range(groups))
     return pl.pallas_call(
         functools.partial(attend_kernel, per_group=per_group, groups=groups),
-        in_specs=[smem, smem, vmem, vmem],
+        in_specs=[smem, smem, pl.BlockSpec(memory_space=pl.ANY), vmem],
         out_specs=[vmem, vmem],
         out_shape=[
             jax.ShapeDtypeStruct((length, dim), jnp.bfloat16),
             jax.ShapeDtypeStruct((groups, dim), jnp.float32),
         ],
         scratch_shapes=[
+            pltpu.VMEM(qkv.shape, jnp.bfloat16),
             pltpu.VMEM((length, dim), jnp.bfloat16),
             pltpu.VMEM((padded, dim), jnp.bfloat16),
             pltpu.VMEM((padded, dim), jnp.bfloat16),
-            pltpu.VMEM((groups + CHUNK, rows, rows), jnp.float32),
+            pltpu.VMEM((most, rows, CHUNK * rows), jnp.float32),
+            pltpu.VMEM((rows, 128), jnp.float32),
+            pltpu.VMEM((rows, 128), jnp.float32),
+            pltpu.VMEM((rows, 128), jnp.float32),
+            pltpu.SMEM((most,), jnp.int32),
+            pltpu.SMEM((most,), jnp.int32),
+            pltpu.SemaphoreType.DMA((4,)),
         ],
-        compiler_params=pltpu.CompilerParams(vmem_limit_bytes=40 * 1024 * 1024),
-        cost_estimate=pl.CostEstimate(
-            flops=4 * length * length * dim, bytes_accessed=4 * length * dim * 2, transcendentals=length * length
-        ),
-    )(place, start, qkv, gate)
+        compiler_params=pltpu.CompilerParams(vmem_limit_bytes=50 * 1024 * 1024),
+    )(order, start, qkv, gate)
 
 
 def combine_kernel(when, attn, square, *refs, per_group):
     parts, out, sums = refs[:-2], refs[-2], refs[-1]
-    block_len, _ = parts[0].shape[1:]
-    sums[...] = square[...]
+    block_len, dim = parts[0].shape[1:]
     at = 0
     for part in parts:
         for k in range(part.shape[0]):
@@ -155,10 +231,11 @@
             at += 1
             rows = pl.ds(pl.multiple_of(t * block_len, block_len), block_len)
             product = attn[rows, :].astype(jnp.float32) * part[k].astype(jnp.float32)
-            row = pl.ds(t // per_group, 1)
-            sums[row, :] = sums[row, :] + jnp.sum(product, axis=0, keepdims=True)
+            sums[pl.ds(t, 1), :] = jnp.sum(product, axis=0, keepdims=True)
+    groups = square.shape[0]
+    total = square[...] + jnp.sum(sums[...].reshape(groups, per_group, dim), axis=1)
     for copy in range(out.shape[0]):
-        out[copy] = sums[...]
+        out[copy] = total
 
 
 def combine(when, attn, square, parts, copies, per_group):
@@ -169,7 +246,7 @@
         in_specs=[smem, vmem, vmem] + [vmem] * len(parts),
         out_specs=vmem,
         out_shape=jax.ShapeDtypeStruct((copies, *square.shape), jnp.float32),
-        scratch_shapes=[pltpu.VMEM(square.shape, jnp.float32)],
+        scratch_shapes=[pltpu.VMEM((square.shape[0] * per_group, square.shape[1]), jnp.float32)],
         compiler_params=pltpu.CompilerParams(vmem_limit_bytes=16 * 1024 * 1024),
     )(when, attn, square, *parts)
 
@@ -249,7 +326,7 @@
     stream = lax.axis_index("stream")
     qkv = to_panels(panels_kernel, (query[0], key[0], value[0]), frames, 3)
     qkv = exchange(qkv, "frame")
-    diff = to_panels(difference_kernel, (latent[0], target[0]), frames, 1)
+    diff = to_panels(difference_kernel, (latent[0], target[0]), frames, 1, 16 * 1024 * 1024)
     parts, masks = exchange_by_swaps(diff, index)
     noise = noise_level
     for mask in (1, 2, 4):
@@ -264,11 +341,10 @@
         embed_own, weight_rows, (((1,), (1,)), ((), ())), preferred_element_type=jnp.float32
     )
     times = jnp.arange(blocks, dtype=jnp.int32)
-    place = jnp.sum(jnp.where(block_order[None, :] == times[:, None], times[None, :], 0), axis=1)
     slots = jnp.array([2 * m + b for m in masks for b in range(2)], jnp.int32) ^ (2 * index)
     when = jnp.sum(jnp.where(slots[:, None] == times[None, :], block_order[None, :], 0), axis=1)
     attn, square = attend(
-        place, context_start[0], qkv.reshape(frames * 6, block_len, local_width), gate, per_group, groups
+        block_order, context_start[0], qkv.reshape(frames * 6, block_len, local_width), gate, per_group, groups
     )
     parts = [p.reshape(-1, block_len, local_width) for p in parts]
     sums = combine(when, attn, square, parts, streams, per_group)

time: 146 us -> 139 us (0.952)
  Pallas kernels: 38.4 us -> 28.5 us
  waiting for transfers between devices: 60.9 us -> 63.5 us
  local copies, waits for them, and re-layouts: 2.2 us -> 4.3 us
    pallas_call x1, Pallas kernels: 27.7 us -> 22.1 us  [attend(): pl.pallas_call(functools.partial(attend_kernel, per_group=per_group, grou...]
    pallas_call x2, Pallas kernels: 8.15 us -> 3.9 us  [to_panels(): pl.pallas_call(functools.partial(kernel, panel=panel), grid=(frames // st...]
    ppermute x13, waiting for transfers between devices: 54.6 us -> 57.2 us  [swap(): return lax.ppermute(value, axis, pairs)]
    unnamed x10 -> x14, local copies, waits for them, and re-layouts: 0.05 us -> 2.48 us
  transfers between devices with their start and end apart: 15 -> 15, of which waited for: 7 -> 7; matrix products, arithmetic and copies ran while one was open for 3% -> 2% of each run, Pallas kernels for 22% -> 16%
where the time goes in v2:
time: 139 us
  waiting for transfers between devices  63.5 us (46%)
  starting transfers between devices  41.5 us (30%)
  Pallas kernels  28.5 us (21%)
  local copies, waits for them, and re-layouts  4.3 us (3%)
    ppermute x13, waiting for transfers between devices, swap(): return lax.ppermute(value, axis, pairs)  57.2 us
    ppermute x13, starting transfers between devices, swap(): return lax.ppermute(value, axis, pairs)  25 us
    pallas_call x1, Pallas kernels, attend(): pl.pallas_call(functools.partial(attend_kernel, per_group=per_group, grou...  22.1 us
    all_to_all x2, starting transfers between devices, exchange(): return lax.all_to_all(value, axis, split_axis=0, concat_axis=0, tiled=True)  16.6 us
    all_to_all x2, waiting for transfers between devices, exchange(): return lax.all_to_all(value, axis, split_axis=0, concat_axis=0, tiled=True)  6.34 us
    pallas_call x2, Pallas kernels, to_panels(): pl.pallas_call(functools.partial(kernel, panel=panel), grid=(frames // st...  3.9 us
  transfers between devices with their start and end apart: 15, of which 7 were waited for; matrix products, arithmetic and copies ran while one was open for 2% of the time, Pallas kernels for 16%

profile of v2, /device:TPU:48, one launch (start us, length us, event | category | flops | bytes accessed | tf_op | source)
XLA Modules:
  0.0 139.1 jit_solution(5614948707475630819)
XLA Ops:
  0.0 0.0 copy-start
  0.0 3.5 %shard_map.100 = bf16[32,384,128]{2,1,0:T(8,128)(2,1)} custom-call(bf16[128,4096]{1,0:T(8,128)(2,1)} %bitcast.57, bf16[128,4096]{1,0:T(8,128)(2,1)} %bitcast.58, bf16[128,4096]{1,0:T(8,128)(2,1)} %bitcast.59), custom_call_target="tpu_custom_call" | custom-call | tf_op jit(solution)/shard_map/pallas_call | solution.py:35
  3.5 11.2 %all-to-all-start = ((bf16[32,384,128]{2,1,0:T(8,128)(2,1)}), bf16[32,384,128]{2,1,0:T(8,128)(2,1)}, u32[]{:S(2)}, u32[]{:S(2)}) async-start(bf16[32,384,128]{2,1,0:T(8,128)(2,1)} %shard_map.100), calls=%async_computation | async-start | bytes 6291456 | tf_op jit(solution)/shard_map/all_to_all | solution.py:283
  14.7 0.0 copy-start.1
  14.7 1.2 copy-done.1
  15.9 0.0 copy-start.2
  15.9 1.2 copy-done.2
  17.1 0.0 copy-start.5
  17.1 0.0 copy-start.6
  17.1 0.0 copy-start.3
  17.1 0.4 shard_map.102
  17.6 0.9 dynamic-slice_bitcast_fusion.3
  18.5 0.3 collective-permute-start.2
  18.8 3.0 %collective-permute-start.1 = (bf16[8,128,128]{2,1,0:T(8,128)(2,1)}, bf16[8,128,128]{2,1,0:T(8,128)(2,1)S(1)}, u32[]{:S(2)}, u32[]{:S(2)}) collective-permute-start(bf16[8,128,128]{2,1,0:T(8,128)(2,1)} %get-tuple-element.19), channel_id=1, source_target_pairs={{0,128},{8,136},{16,144},{24,152},{32,160},{40,168},{48,176},{56,1... | collective-permute-start | bytes 786440 | tf_op jit(solution)/shard_map/ppermute | solution.py:288
  21.8 0.1 collective-permute-start
  21.9 0.0 copy-done.5
  21.9 1.5 %collective-permute-start.10 = (f32[1,16]{1,0:T(1,128)S(1)}, f32[1,16]{1,0:T(1,128)S(1)}, u32[]{:S(2)}, u32[]{:S(2)}) collective-permute-start(f32[1,16]{1,0:T(1,128)S(1)} %copy-done.5), channel_id=1, source_target_pairs={{0,1},{1,0},{2,3},{3,2},{4,5},{5,4},{6,7},{7,6},{8,9},{9,8},{10,11... | collective-permute-start | bytes 200 | tf_op jit(solution)/shard_map/ppermute | solution.py:288
  23.4 0.1 fusion.4
  23.5 0.0 copy-done
  23.6 0.1 fusion.2.gate
  23.7 0.0 copy-done.6
  23.7 0.0 copy-done.3
  23.7 0.2 select_reduce_fusion.1.when
  23.9 1.6 %collective-permute-done.10 = f32[1,16]{1,0:T(1,128)S(1)} collective-permute-done((f32[1,16]{1,0:T(1,128)S(1)}, f32[1,16]{1,0:T(1,128)S(1)}, u32[]{:S(2)}, u32[]{:S(2)}) %collective-permute-start.10) | collective-permute-done | bytes 96 | tf_op jit(solution)/shard_map/ppermute | solution.py:288
  25.5 3.1 %collective-permute-start.11 = (f32[2,16]{1,0:T(2,128)S(1)}, f32[2,16]{1,0:T(2,128)S(1)}, u32[]{:S(2)}, u32[]{:S(2)}) collective-permute-start(f32[2,16]{1,0:T(2,128)S(1)} %pad_maximum_fusion.3), channel_id=1, source_target_pairs={{0,2},{1,3},{2,0},{3,1},{4,6},{5,7},{6,4},{7,5},{8,10},{9,11},{10,... | collective-permute-start | bytes 392 | tf_op jit(solution)/shard_map/ppermute | solution.py:288
  28.6 2.1 %collective-permute-done.11 = f32[2,16]{1,0:T(2,128)S(1)} collective-permute-done((f32[2,16]{1,0:T(2,128)S(1)}, f32[2,16]{1,0:T(2,128)S(1)}, u32[]{:S(2)}, u32[]{:S(2)}) %collective-permute-start.11) | collective-permute-done | bytes 160 | tf_op jit(solution)/shard_map/ppermute | solution.py:288
  30.7 1.4 collective-permute-start.12
  32.0 7.8 %collective-permute-done.12 = f32[4,16]{1,0:T(4,128)S(1)} collective-permute-done((f32[4,16]{1,0:T(4,128)S(1)}, f32[4,16]{1,0:T(4,128)S(1)}, u32[]{:S(2)}, u32[]{:S(2)}) %collective-permute-start.12) | collective-permute-done | bytes 288 | tf_op jit(solution)/shard_map/ppermute | solution.py:288
  39.8 0.1 select_reduce_fusion
  39.9 0.0 collective-permute-done.2
  40.0 7.8 %collective-permute-done.1 = bf16[8,128,128]{2,1,0:T(8,128)(2,1)S(1)} collective-permute-done((bf16[8,128,128]{2,1,0:T(8,128)(2,1)}, bf16[8,128,128]{2,1,0:T(8,128)(2,1)S(1)}, u32[]{:S(2)}, u32[]{:S(2)}) %collective-permute-start.1) | collective-permute-done | bytes 262176 | tf_op jit(solution)/shard_map/ppermute | solution.py:288
  47.7 0.0 collective-permute-done
  47.7 0.0 copy-start.4
  47.7 0.1 pad_maximum_fusion
  47.8 0.8 dynamic-slice_bitcast_fusion.4
  48.6 0.0 collective-permute-start.3
  48.6 0.0 collective-permute-start.4
  48.6 0.1 mul.69
  48.7 3.5 %collective-permute-start.5 = (bf16[4,128,128]{2,1,0:T(8,128)(2,1)}, bf16[4,128,128]{2,1,0:T(8,128)(2,1)S(1)}, u32[]{:S(2)}, u32[]{:S(2)}) collective-permute-start(bf16[4,128,128]{2,1,0:T(8,128)(2,1)} %get-tuple-element.13), channel_id=1, source_target_pairs={{0,48},{8,56},{16,32},{24,40},{32,16},{40,24},{48,0},{56,8},{64,11... | collective-permute-start | bytes 393224 | tf_op jit(solution)/shard_map/ppermute | solution.py:288
  52.2 1.5 %collective-permute-start.6 = (bf16[4,128,128]{2,1,0:T(8,128)(2,1)}, bf16[4,128,128]{2,1,0:T(8,128)(2,1)S(1)}, u32[]{:S(2)}, u32[]{:S(2)}) collective-permute-start(bf16[4,128,128]{2,1,0:T(8,128)(2,1)} %get-tuple-element.12), channel_id=1, source_target_pairs={{0,64},{8,72},{16,80},{24,88},{32,96},{40,104},{48,112},{56,120},{... | collective-permute-start | bytes 393224 | tf_op jit(solution)/shard_map/ppermute | solution.py:288
  53.8 3.8 %collective-permute-start.7 = (bf16[4,128,128]{2,1,0:T(8,128)(2,1)}, bf16[4,128,128]{2,1,0:T(8,128)(2,1)S(1)}, u32[]{:S(2)}, u32[]{:S(2)}) collective-permute-start(bf16[4,128,128]{2,1,0:T(8,128)(2,1)} %get-tuple-element.11), channel_id=1, source_target_pairs={{0,80},{8,88},{16,64},{24,72},{32,112},{40,120},{48,96},{56,104},{... | collective-permute-start | bytes 393224 | tf_op jit(solution)/shard_map/ppermute | solution.py:288
  57.6 34.1 %collective-permute-done.3 = bf16[4,128,128]{2,1,0:T(8,128)(2,1)S(1)} collective-permute-done((bf16[4,128,128]{2,1,0:T(8,128)(2,1)S(1)}, bf16[4,128,128]{2,1,0:T(8,128)(2,1)S(1)}, u32[]{:S(2)}, u32[]{:S(2)}) %collective-permute-start.3) | collective-permute-done | bytes 131104 | tf_op jit(solution)/shard_map/ppermute | solution.py:288
  91.7 1.7 %collective-permute-start.8 = (bf16[4,128,128]{2,1,0:T(8,128)(2,1)S(1)}, bf16[4,128,128]{2,1,0:T(8,128)(2,1)S(1)}, u32[]{:S(2)}, u32[]{:S(2)}) collective-permute-start(bf16[4,128,128]{2,1,0:T(8,128)(2,1)S(1)} %get-tuple-element.10), channel_id=1, source_target_pairs={{0,96},{8,104},{16,112},{24,120},{32,64},{40,72},{48,80},{56,88},{... | collective-permute-start | bytes 393224 | tf_op jit(solution)/shard_map/ppermute | solution.py:288
  93.4 4.0 %collective-permute-done.4 = bf16[4,128,128]{2,1,0:T(8,128)(2,1)S(1)} collective-permute-done((bf16[4,128,128]{2,1,0:T(8,128)(2,1)S(1)}, bf16[4,128,128]{2,1,0:T(8,128)(2,1)S(1)}, u32[]{:S(2)}, u32[]{:S(2)}) %collective-permute-start.4) | collective-permute-done | bytes 131104 | tf_op jit(solution)/shard_map/ppermute | solution.py:288
  97.4 5.0 %collective-permute-start.9 = (bf16[4,128,128]{2,1,0:T(8,128)(2,1)S(1)}, bf16[4,128,128]{2,1,0:T(8,128)(2,1)S(1)}, u32[]{:S(2)}, u32[]{:S(2)}) collective-permute-start(bf16[4,128,128]{2,1,0:T(8,128)(2,1)S(1)} %get-tuple-element.9), channel_id=1, source_target_pairs={{0,112},{8,120},{16,96},{24,104},{32,80},{40,88},{48,64},{56,72},{... | collective-permute-start | bytes 393224 | tf_op jit(solution)/shard_map/ppermute | solution.py:288
  102.4 0.3 fusion
  102.7 0.0 all-to-all-done
  102.7 0.0 copy-done.4
  102.7 22.1 %shard_map.101 = (bf16[4096,128]{1,0:T(8,128)(2,1)S(1)}, f32[16,128]{1,0:T(8,128)S(1)}) custom-call(s32[64]{0:T(128)S(1)} %copy-done.3, s32[16]{0:T(128)S(1)} %bitcast.56, bf16[192,64,128]{2,1,0:T(8,128)(2,1)} %bitcast.4.qkv, f32[16,128]{1,0:T(8,128)S(1)} %fusion.2.gate), custom_call_target="tpu_custom_call" | custom-call | tf_op jit(solution)/shard_map/pallas_call | solution.py:199
  124.8 0.0 collective-permute-done.5
  124.8 0.0 collective-permute-done.6
  124.8 0.0 collective-permute-done.7
  124.8 0.0 collective-permute-done.8
  124.8 0.0 collective-permute-done.9
  124.8 1.5 %shard_map.103 = f32[8,16,128]{2,1,0:T(8,128)} custom-call(s32[64]{0:T(128)S(1)} %select_reduce_fusion.1.when, bf16[4096,128]{1,0:T(8,128)(2,1)S(1)} %get-tuple-element.7.attn, f32[16,128]{1,0:T(8,128)S(1)} %get-tuple-element.8.square, bf16[8,64,128]{2,1,0:T(8,128)(2,1)S(1)} %bitcast.47, bf16[8,64,128]{2,1,0:T(8,128)(2,1)S(1)} %bitcast.49, ...), custom_call_target="tpu_custom_call" | custom-call | tf_op jit(solution)/shard_map/pallas_call | solution.py:244
  126.4 5.4 %all-to-all-start.1 = ((f32[8,16,128]{2,1,0:T(8,128)}), f32[8,16,128]{2,1,0:T(8,128)S(1)}, u32[]{:S(2)}, u32[]{:S(2)}) async-start(f32[8,16,128]{2,1,0:T(8,128)} %shard_map.103), calls=%async_computation.1 | async-start | bytes 131072 | tf_op jit(solution)/shard_map/all_to_all | solution.py:283
  131.8 6.3 %all-to-all-done.1 = f32[8,16,128]{2,1,0:T(8,128)S(1)} async-done(((f32[8,16,128]{2,1,0:T(8,128)}), f32[8,16,128]{2,1,0:T(8,128)S(1)}, u32[]{:S(2)}, u32[]{:S(2)}) %all-to-all-start.1) | async-done | bytes 65568 | tf_op jit(solution)/shard_map/all_to_all | solution.py:283
  138.1 1.0 shard_map.104
  (10 shorter events, 0.1 us)
Async XLA Ops:
  0.0 23.5 %copy-start = (bf16[4096,256]{1,0:T(8,128)(2,1)S(1)}, bf16[4096,256]{1,0:T(8,128)(2,1)}, u32[]{:S(2)}) copy-start(bf16[4096,256]{1,0:T(8,128)(2,1)} %param.16) | copy-start | bytes 6291460
  3.5 99.2 %all-to-all-start = ((bf16[32,384,128]{2,1,0:T(8,128)(2,1)}), bf16[32,384,128]{2,1,0:T(8,128)(2,1)}, u32[]{:S(2)}, u32[]{:S(2)}) async-start(bf16[32,384,128]{2,1,0:T(8,128)(2,1)} %shard_map.100), calls=%async_computation | async-start | bytes 6291456 | tf_op jit(solution)/shard_map/all_to_all | solution.py:283
  14.7 1.2 copy-start.1
  15.9 1.2 copy-start.2
  17.1 4.8 %copy-start.5 = (f32[1,16]{1,0:T(1,128)S(1)}, f32[1,16]{1,0:T(1,128)}, u32[]{:S(2)}) copy-start(f32[1,16]{1,0:T(1,128)} %param.15) | copy-start | bytes 196
  17.1 6.6 %copy-start.6 = (s32[64]{0:T(128)S(1)}, s32[64]{0:T(128)}, u32[]{:S(2)}) copy-start(s32[64]{0:T(128)} %constant.60.clone) | copy-start | bytes 772
  17.1 6.6 %copy-start.3 = (s32[64]{0:T(128)S(1)}, s32[64]{0:T(128)}, u32[]{:S(2)}) copy-start(s32[64]{0:T(128)} %order.1) | copy-start | bytes 772
  18.5 21.4 %collective-permute-start.2 = (bf16[8,128,128]{2,1,0:T(8,128)(2,1)}, bf16[8,128,128]{2,1,0:T(8,128)(2,1)S(1)}, u32[]{:S(2)}, u32[]{:S(2)}) collective-permute-start(bf16[8,128,128]{2,1,0:T(8,128)(2,1)} %get-tuple-element.18), channel_id=1, source_target_pairs={{0,136},{8,128},{16,152},{24,144},{32,168},{40,160},{48,184},{56,1... | collective-permute-start | bytes 786440 | tf_op jit(solution)/shard_map/ppermute | solution.py:288
  18.8 28.9 %collective-permute-start.1 = (bf16[8,128,128]{2,1,0:T(8,128)(2,1)}, bf16[8,128,128]{2,1,0:T(8,128)(2,1)S(1)}, u32[]{:S(2)}, u32[]{:S(2)}) collective-permute-start(bf16[8,128,128]{2,1,0:T(8,128)(2,1)} %get-tuple-element.19), channel_id=1, source_target_pairs={{0,128},{8,136},{16,144},{24,152},{32,160},{40,168},{48,176},{56,1... | collective-permute-start | bytes 786440 | tf_op jit(solution)/shard_map/ppermute | solution.py:288
  21.8 25.9 %collective-permute-start = (bf16[8,128,128]{2,1,0:T(8,128)(2,1)}, bf16[8,128,128]{2,1,0:T(8,128)(2,1)S(1)}, u32[]{:S(2)}, u32[]{:S(2)}) collective-permute-start(bf16[8,128,128]{2,1,0:T(8,128)(2,1)} %get-tuple-element.20), channel_id=1, source_target_pairs={{0,8},{8,0},{16,24},{24,16},{32,40},{40,32},{48,56},{56,48},{64,72... | collective-permute-start | bytes 786440 | tf_op jit(solution)/shard_map/ppermute | solution.py:288
  21.9 3.6 %collective-permute-start.10 = (f32[1,16]{1,0:T(1,128)S(1)}, f32[1,16]{1,0:T(1,128)S(1)}, u32[]{:S(2)}, u32[]{:S(2)}) collective-permute-start(f32[1,16]{1,0:T(1,128)S(1)} %copy-done.5), channel_id=1, source_target_pairs={{0,1},{1,0},{2,3},{3,2},{4,5},{5,4},{6,7},{7,6},{8,9},{9,8},{10,11... | collective-permute-start | bytes 200 | tf_op jit(solution)/shard_map/ppermute | solution.py:288
  25.5 5.2 %collective-permute-start.11 = (f32[2,16]{1,0:T(2,128)S(1)}, f32[2,16]{1,0:T(2,128)S(1)}, u32[]{:S(2)}, u32[]{:S(2)}) collective-permute-start(f32[2,16]{1,0:T(2,128)S(1)} %pad_maximum_fusion.3), channel_id=1, source_target_pairs={{0,2},{1,3},{2,0},{3,1},{4,6},{5,7},{6,4},{7,5},{8,10},{9,11},{10,... | collective-permute-start | bytes 392 | tf_op jit(solution)/shard_map/ppermute | solution.py:288
  30.7 9.2 %collective-permute-start.12 = (f32[4,16]{1,0:T(4,128)S(1)}, f32[4,16]{1,0:T(4,128)S(1)}, u32[]{:S(2)}, u32[]{:S(2)}) collective-permute-start(f32[4,16]{1,0:T(4,128)S(1)} %pad_maximum_fusion.2), channel_id=1, source_target_pairs={{0,4},{1,5},{2,6},{3,7},{4,0},{5,1},{6,2},{7,3},{8,12},{9,13},{10,... | collective-permute-start | bytes 776 | tf_op jit(solution)/shard_map/ppermute | solution.py:288
  47.7 55.0 %copy-start.4 = (s32[1,16]{1,0:T(1,128)S(1)}, s32[1,16]{1,0:T(1,128)}, u32[]{:S(2)}) copy-start(s32[1,16]{1,0:T(1,128)} %param.18) | copy-start | bytes 196
  48.6 43.0 %collective-permute-start.3 = (bf16[4,128,128]{2,1,0:T(8,128)(2,1)S(1)}, bf16[4,128,128]{2,1,0:T(8,128)(2,1)S(1)}, u32[]{:S(2)}, u32[]{:S(2)}) collective-permute-start(bf16[4,128,128]{2,1,0:T(8,128)(2,1)S(1)} %get-tuple-element.15), channel_id=1, source_target_pairs={{0,16},{8,24},{16,0},{24,8},{32,48},{40,56},{48,32},{56,40},{64,80... | collective-permute-start | bytes 393224 | tf_op jit(solution)/shard_map/ppermute | solution.py:288
  48.6 48.7 %collective-permute-start.4 = (bf16[4,128,128]{2,1,0:T(8,128)(2,1)S(1)}, bf16[4,128,128]{2,1,0:T(8,128)(2,1)S(1)}, u32[]{:S(2)}, u32[]{:S(2)}) collective-permute-start(bf16[4,128,128]{2,1,0:T(8,128)(2,1)S(1)} %get-tuple-element.14), channel_id=1, source_target_pairs={{0,32},{8,40},{16,48},{24,56},{32,0},{40,8},{48,16},{56,24},{64,96... | collective-permute-start | bytes 393224 | tf_op jit(solution)/shard_map/ppermute | solution.py:288
  48.7 76.0 %collective-permute-start.5 = (bf16[4,128,128]{2,1,0:T(8,128)(2,1)}, bf16[4,128,128]{2,1,0:T(8,128)(2,1)S(1)}, u32[]{:S(2)}, u32[]{:S(2)}) collective-permute-start(bf16[4,128,128]{2,1,0:T(8,128)(2,1)} %get-tuple-element.13), channel_id=1, source_target_pairs={{0,48},{8,56},{16,32},{24,40},{32,16},{40,24},{48,0},{56,8},{64,11... | collective-permute-start | bytes 393224 | tf_op jit(solution)/shard_map/ppermute | solution.py:288
  52.2 72.5 %collective-permute-start.6 = (bf16[4,128,128]{2,1,0:T(8,128)(2,1)}, bf16[4,128,128]{2,1,0:T(8,128)(2,1)S(1)}, u32[]{:S(2)}, u32[]{:S(2)}) collective-permute-start(bf16[4,128,128]{2,1,0:T(8,128)(2,1)} %get-tuple-element.12), channel_id=1, source_target_pairs={{0,64},{8,72},{16,80},{24,88},{32,96},{40,104},{48,112},{56,120},{... | collective-permute-start | bytes 393224 | tf_op jit(solution)/shard_map/ppermute | solution.py:288
  53.8 71.0 %collective-permute-start.7 = (bf16[4,128,128]{2,1,0:T(8,128)(2,1)}, bf16[4,128,128]{2,1,0:T(8,128)(2,1)S(1)}, u32[]{:S(2)}, u32[]{:S(2)}) collective-permute-start(bf16[4,128,128]{2,1,0:T(8,128)(2,1)} %get-tuple-element.11), channel_id=1, source_target_pairs={{0,80},{8,88},{16,64},{24,72},{32,112},{40,120},{48,96},{56,104},{... | collective-permute-start | bytes 393224 | tf_op jit(solution)/shard_map/ppermute | solution.py:288
  91.7 33.1 %collective-permute-start.8 = (bf16[4,128,128]{2,1,0:T(8,128)(2,1)S(1)}, bf16[4,128,128]{2,1,0:T(8,128)(2,1)S(1)}, u32[]{:S(2)}, u32[]{:S(2)}) collective-permute-start(bf16[4,128,128]{2,1,0:T(8,128)(2,1)S(1)} %get-tuple-element.10), channel_id=1, source_target_pairs={{0,96},{8,104},{16,112},{24,120},{32,64},{40,72},{48,80},{56,88},{... | collective-permute-start | bytes 393224 | tf_op jit(solution)/shard_map/ppermute | solution.py:288
  97.4 27.4 %collective-permute-start.9 = (bf16[4,128,128]{2,1,0:T(8,128)(2,1)S(1)}, bf16[4,128,128]{2,1,0:T(8,128)(2,1)S(1)}, u32[]{:S(2)}, u32[]{:S(2)}) collective-permute-start(bf16[4,128,128]{2,1,0:T(8,128)(2,1)S(1)} %get-tuple-element.9), channel_id=1, source_target_pairs={{0,112},{8,120},{16,96},{24,104},{32,80},{40,88},{48,64},{56,72},{... | collective-permute-start | bytes 393224 | tf_op jit(solution)/shard_map/ppermute | solution.py:288
  126.4 11.7 %all-to-all-start.1 = ((f32[8,16,128]{2,1,0:T(8,128)}), f32[8,16,128]{2,1,0:T(8,128)S(1)}, u32[]{:S(2)}, u32[]{:S(2)}) async-start(f32[8,16,128]{2,1,0:T(8,128)} %shard_map.103), calls=%async_computation.1 | async-start | bytes 131072 | tf_op jit(solution)/shard_map/all_to_all | solution.py:283

commit v3 on v2

--- a/solution.py
+++ b/solution.py
@@ -9,7 +9,8 @@
 from jax.sharding import PartitionSpec as P
 
 
-CHUNK = 4
+CHUNK = 3
+LIMIT = 52 * 1024 * 1024
 ROWS = 32
 
 
@@ -53,7 +54,8 @@
     q_sorted,
     k_sorted,
     v_sorted,
-    strip,
+    even,
+    odd,
     levels,
     tops,
     totals,
@@ -88,6 +90,14 @@
         return lax.fori_loop(0, (c - start[c] + CHUNK) // CHUNK, list_chunk, at)
 
     chunks = lax.fori_loop(0, groups, list_group, 0)
+    filler = jnp.minimum(chunks, group_of.shape[0] - 1)
+    steps = (chunks + 1) // 2
+
+    @pl.when(chunks % 2 == 1)
+    def _():
+        group_of[filler] = groups - 1
+        tile_of[filler] = groups
+
 
     pad = jnp.zeros(((CHUNK - 1) * rows, dim), jnp.bfloat16)
     k_sorted[blocks * block_len :, :] = pad
@@ -108,9 +118,11 @@
         lax.fori_loop(n * per_piece, (n + 1) * per_piece, sort_block, 0, unroll=8)
 
     def rows_of(ref, tile, count):
+        tile = jnp.minimum(tile, groups - 1)
         return ref[pl.ds(pl.multiple_of(tile * rows, rows), count), :]
 
-    def scores(t):
+    def scores(t, strip, slot):
+        t = jnp.minimum(t, 2 * steps - 1)
         c, tile = group_of[t], tile_of[t]
         s = lax.dot_general(
             rows_of(q_sorted, c, rows),
@@ -118,19 +130,19 @@
             (((1,), (1,)), ((), ())),
             preferred_element_type=jnp.float32,
         )
-        strip[t] = s
-
-    def normalize(t):
+        strip[slot] = s
+
+    def normalize(t, strip, slot):
         c, tile = group_of[t], tile_of[t]
         fresh = tile == start[c]
         for r in range(0, rows, ROWS):
             at_r = slice(r, r + ROWS)
-            peak = None
+            peak = jnp.full((ROWS, 128), -jnp.inf, jnp.float32)
             for u in range(CHUNK):
-                top = strip[t, at_r, u * rows : u * rows + 128]
+                top = strip[slot, at_r, u * rows : u * rows + 128]
                 for b in range(1, rows // 128):
-                    top = jnp.maximum(top, strip[t, at_r, u * rows + b * 128 : u * rows + (b + 1) * 128])
-                peak = top if u == 0 else jnp.maximum(peak, jnp.where(tile + u <= c, top, -jnp.inf))
+                    top = jnp.maximum(top, strip[slot, at_r, u * rows + b * 128 : u * rows + (b + 1) * 128])
+                peak = jnp.maximum(peak, jnp.where(tile + u <= c, top, -jnp.inf))
             peak = jnp.broadcast_to(jnp.max(peak, axis=1, keepdims=True) * factor, (ROWS, 128))
             before = jnp.where(fresh, -jnp.inf, tops[at_r, :])
             top = jnp.maximum(before, peak)
@@ -139,30 +151,31 @@
                 here = jnp.where(tile + u <= c, top, jnp.inf)
                 for b in range(rows // 128):
                     at = u * rows + b * 128
-                    total = total + jnp.exp2(strip[t, at_r, at : at + 128] * factor - here)
+                    total = total + jnp.exp2(strip[slot, at_r, at : at + 128] * factor - here)
             tops[at_r, :] = top
             totals[at_r, :] = total
             level = top + jnp.log2(jnp.sum(total, axis=1, keepdims=True))
             lanes = lax.broadcasted_iota(jnp.int32, (ROWS, 128), 1)
             levels[at_r, :] = jnp.where(lanes == c, level, levels[at_r, :])
 
-    def first_pass(t, carry):
-        normalize(t - 1)
-        scores(t)
+    def first_pass(i, carry):
+        normalize(2 * i, even, i)
+        scores(2 * i + 1, odd, i)
+        normalize(2 * i + 1, odd, i)
+        scores(2 * i + 2, even, i + 1)
         return carry
 
     totals[...] = jnp.zeros(totals.shape, jnp.float32)
     tops[...] = jnp.zeros(tops.shape, jnp.float32)
-    scores(0)
-    lax.fori_loop(1, chunks, first_pass, 0)
-    normalize(chunks - 1)
+    scores(0, even, 0)
+    lax.fori_loop(0, steps, first_pass, 0)
 
     def level_of(c):
         lanes = lax.broadcasted_iota(jnp.int32, levels.shape, 1)
         level = jnp.sum(jnp.where(lanes == c, levels[...], 0.0), axis=1, keepdims=True)
         return jnp.broadcast_to(level, (rows, 128))
 
-    def second_pass(t, carry):
+    def weigh(t, strip, slot, carry):
         acc, level = carry
         c, tile = group_of[t], tile_of[t]
         probs = []
@@ -170,14 +183,14 @@
             here = jnp.where(tile + u <= c, level, jnp.inf)
             for b in range(rows // 128):
                 at = u * rows + b * 128
-                probs.append(jnp.exp2(strip[t, :, at : at + 128] * factor - here).astype(jnp.bfloat16))
+                probs.append(jnp.exp2(strip[slot, :, at : at + 128] * factor - here).astype(jnp.bfloat16))
         part = lax.dot_general(
             jnp.concatenate(probs, axis=1),
             rows_of(v_sorted, tile, wide),
             (((1,), (0,)), ((), ())),
             preferred_element_type=jnp.float32,
         )
-        level = level_of(group_of[jnp.minimum(t + 1, chunks - 1)])
+        level = level_of(group_of[jnp.minimum(t + 1, 2 * steps - 1)])
         acc = jnp.where(tile == start[c], 0.0, acc) + part
         rounded = acc.astype(jnp.bfloat16)
         attn_out[pl.ds(pl.multiple_of(c * rows, rows), rows), :] = rounded
@@ -185,7 +198,10 @@
         square_out[pl.ds(c, 1), :] = gate[pl.ds(c, 1), :] * jnp.sum(back * back, axis=0, keepdims=True)
         return acc, level
 
-    lax.fori_loop(0, chunks, second_pass, (jnp.zeros((rows, dim), jnp.float32), level_of(0)))
+    def second_pass(i, carry):
+        return weigh(2 * i + 1, odd, i, weigh(2 * i, even, i, carry))
+
+    lax.fori_loop(0, steps, second_pass, (jnp.zeros((rows, dim), jnp.float32), level_of(0)))
 
 
 def attend(order, start, qkv, gate, per_group, groups):
@@ -196,6 +212,7 @@
     vmem = pl.BlockSpec(memory_space=pltpu.VMEM)
     padded = length + (CHUNK - 1) * rows
     most = sum((c + CHUNK) // CHUNK for c in range(groups))
+    most += most % 2
     return pl.pallas_call(
         functools.partial(attend_kernel, per_group=per_group, groups=groups),
         in_specs=[smem, smem, pl.BlockSpec(memory_space=pl.ANY), vmem],
@@ -209,7 +226,8 @@
             pltpu.VMEM((length, dim), jnp.bfloat16),
             pltpu.VMEM((padded, dim), jnp.bfloat16),
             pltpu.VMEM((padded, dim), jnp.bfloat16),
-            pltpu.VMEM((most, rows, CHUNK * rows), jnp.float32),
+            pltpu.VMEM((most // 2 + 1, rows, CHUNK * rows), jnp.float32),
+            pltpu.VMEM((most // 2, rows, CHUNK * rows), jnp.float32),
             pltpu.VMEM((rows, 128), jnp.float32),
             pltpu.VMEM((rows, 128), jnp.float32),
             pltpu.VMEM((rows, 128), jnp.float32),
@@ -217,7 +235,7 @@
             pltpu.SMEM((most,), jnp.int32),
             pltpu.SemaphoreType.DMA((4,)),
         ],
-        compiler_params=pltpu.CompilerParams(vmem_limit_bytes=50 * 1024 * 1024),
+        compiler_params=pltpu.CompilerParams(vmem_limit_bytes=LIMIT),
     )(order, start, qkv, gate)
 
 

time: 139 us -> 138 us (level)
  the two profiles are of different devices: /device:TPU:48 before, /device:TPU:96 now
where the time goes in v3:
time: 138 us
  waiting for transfers between devices  57.9 us (42%)
  starting transfers between devices  46.3 us (34%)
  Pallas kernels  27.9 us (20%)
  local copies, waits for them, and re-layouts  4.3 us (3%)
    ppermute x13, waiting for transfers between devices, swap(): return lax.ppermute(value, axis, pairs)  51.6 us
    ppermute x13, starting transfers between devices, swap(): return lax.ppermute(value, axis, pairs)  31.6 us
    pallas_call x1, Pallas kernels, attend(): pl.pallas_call(functools.partial(attend_kernel, per_group=per_group, grou...  21.5 us
    all_to_all x2, starting transfers between devices, exchange(): return lax.all_to_all(value, axis, split_axis=0, concat_axis=0, tiled=True)  14.7 us
    all_to_all x2, waiting for transfers between devices, exchange(): return lax.all_to_all(value, axis, split_axis=0, concat_axis=0, tiled=True)  6.34 us
    pallas_call x2, Pallas kernels, to_panels(): pl.pallas_call(functools.partial(kernel, panel=panel), grid=(frames // st...  3.9 us
  transfers between devices with their start and end apart: 15, of which 5 were waited for; matrix products, arithmetic and copies ran while one was open for 2% of the time, Pallas kernels for 16%

profile of v3, /device:TPU:96, one launch (start us, length us, event | category | flops | bytes accessed | tf_op | source)
XLA Modules:
  0.0 137.8 jit_solution(8070299170600741491)
XLA Ops:
  0.0 0.0 copy-start
  0.0 3.5 %shard_map.100 = bf16[32,384,128]{2,1,0:T(8,128)(2,1)} custom-call(bf16[128,4096]{1,0:T(8,128)(2,1)} %bitcast.57, bf16[128,4096]{1,0:T(8,128)(2,1)} %bitcast.58, bf16[128,4096]{1,0:T(8,128)(2,1)} %bitcast.59), custom_call_target="tpu_custom_call" | custom-call | tf_op jit(solution)/shard_map/pallas_call | solution.py:36
  3.5 10.5 %all-to-all-start = ((bf16[32,384,128]{2,1,0:T(8,128)(2,1)}), bf16[32,384,128]{2,1,0:T(8,128)(2,1)}, u32[]{:S(2)}, u32[]{:S(2)}) async-start(bf16[32,384,128]{2,1,0:T(8,128)(2,1)} %shard_map.100), calls=%async_computation | async-start | bytes 6291456 | tf_op jit(solution)/shard_map/all_to_all | solution.py:301
  14.0 0.0 copy-start.1
  14.0 1.2 copy-done.1
  15.2 0.0 copy-start.2
  15.2 1.2 copy-done.2
  16.4 0.0 copy-start.5
  16.4 0.0 copy-start.6
  16.4 0.0 copy-start.3
  16.4 0.4 shard_map.102
  16.9 0.9 dynamic-slice_bitcast_fusion.3
  17.9 2.7 %collective-permute-start.2 = (bf16[8,128,128]{2,1,0:T(8,128)(2,1)}, bf16[8,128,128]{2,1,0:T(8,128)(2,1)S(1)}, u32[]{:S(2)}, u32[]{:S(2)}) collective-permute-start(bf16[8,128,128]{2,1,0:T(8,128)(2,1)} %get-tuple-element.18), channel_id=1, source_target_pairs={{0,136},{8,128},{16,152},{24,144},{32,168},{40,160},{48,184},{56,1... | collective-permute-start | bytes 786440 | tf_op jit(solution)/shard_map/ppermute | solution.py:306
  20.6 0.5 collective-permute-start.1
  21.1 0.1 collective-permute-start
  21.2 0.0 copy-done.5
  21.2 1.5 %collective-permute-start.10 = (f32[1,16]{1,0:T(1,128)S(1)}, f32[1,16]{1,0:T(1,128)S(1)}, u32[]{:S(2)}, u32[]{:S(2)}) collective-permute-start(f32[1,16]{1,0:T(1,128)S(1)} %copy-done.5), channel_id=1, source_target_pairs={{0,1},{1,0},{2,3},{3,2},{4,5},{5,4},{6,7},{7,6},{8,9},{9,8},{10,11... | collective-permute-start | bytes 200 | tf_op jit(solution)/shard_map/ppermute | solution.py:306
  22.7 0.1 fusion.4
  22.9 0.0 copy-done
  22.9 0.1 fusion.2.gate
  23.0 0.0 copy-done.6
  23.0 0.0 copy-done.3
  23.0 0.2 select_reduce_fusion.1.when
  23.2 1.6 %collective-permute-done.10 = f32[1,16]{1,0:T(1,128)S(1)} collective-permute-done((f32[1,16]{1,0:T(1,128)S(1)}, f32[1,16]{1,0:T(1,128)S(1)}, u32[]{:S(2)}, u32[]{:S(2)}) %collective-permute-start.10) | collective-permute-done | bytes 96 | tf_op jit(solution)/shard_map/ppermute | solution.py:306
  24.8 3.1 %collective-permute-start.11 = (f32[2,16]{1,0:T(2,128)S(1)}, f32[2,16]{1,0:T(2,128)S(1)}, u32[]{:S(2)}, u32[]{:S(2)}) collective-permute-start(f32[2,16]{1,0:T(2,128)S(1)} %pad_maximum_fusion.3), channel_id=1, source_target_pairs={{0,2},{1,3},{2,0},{3,1},{4,6},{5,7},{6,4},{7,5},{8,10},{9,11},{10,... | collective-permute-start | bytes 392 | tf_op jit(solution)/shard_map/ppermute | solution.py:306
  27.9 2.1 %collective-permute-done.11 = f32[2,16]{1,0:T(2,128)S(1)} collective-permute-done((f32[2,16]{1,0:T(2,128)S(1)}, f32[2,16]{1,0:T(2,128)S(1)}, u32[]{:S(2)}, u32[]{:S(2)}) %collective-permute-start.11) | collective-permute-done | bytes 160 | tf_op jit(solution)/shard_map/ppermute | solution.py:306
  30.0 0.8 collective-permute-start.12
  30.7 12.5 %collective-permute-done.12 = f32[4,16]{1,0:T(4,128)S(1)} collective-permute-done((f32[4,16]{1,0:T(4,128)S(1)}, f32[4,16]{1,0:T(4,128)S(1)}, u32[]{:S(2)}, u32[]{:S(2)}) %collective-permute-start.12) | collective-permute-done | bytes 288 | tf_op jit(solution)/shard_map/ppermute | solution.py:306
  43.3 0.1 select_reduce_fusion
  43.3 0.0 collective-permute-done.2
  43.4 0.0 collective-permute-done.1
  43.4 0.0 collective-permute-done
  43.4 0.0 copy-start.4
  43.4 0.1 pad_maximum_fusion
  43.5 0.8 dynamic-slice_bitcast_fusion.4
  44.3 1.2 collective-permute-start.3
  45.5 3.3 %collective-permute-start.4 = (bf16[4,128,128]{2,1,0:T(8,128)(2,1)S(1)}, bf16[4,128,128]{2,1,0:T(8,128)(2,1)S(1)}, u32[]{:S(2)}, u32[]{:S(2)}) collective-permute-start(bf16[4,128,128]{2,1,0:T(8,128)(2,1)S(1)} %get-tuple-element.14), channel_id=1, source_target_pairs={{0,32},{8,40},{16,48},{24,56},{32,0},{40,8},{48,16},{56,24},{64,96... | collective-permute-start | bytes 393224 | tf_op jit(solution)/shard_map/ppermute | solution.py:306
  48.8 0.1 mul.69
  48.9 1.5 %collective-permute-start.5 = (bf16[4,128,128]{2,1,0:T(8,128)(2,1)}, bf16[4,128,128]{2,1,0:T(8,128)(2,1)S(1)}, u32[]{:S(2)}, u32[]{:S(2)}) collective-permute-start(bf16[4,128,128]{2,1,0:T(8,128)(2,1)} %get-tuple-element.13), channel_id=1, source_target_pairs={{0,48},{8,56},{16,32},{24,40},{32,16},{40,24},{48,0},{56,8},{64,11... | collective-permute-start | bytes 393224 | tf_op jit(solution)/shard_map/ppermute | solution.py:306
  50.4 4.3 %collective-permute-start.6 = (bf16[4,128,128]{2,1,0:T(8,128)(2,1)}, bf16[4,128,128]{2,1,0:T(8,128)(2,1)S(1)}, u32[]{:S(2)}, u32[]{:S(2)}) collective-permute-start(bf16[4,128,128]{2,1,0:T(8,128)(2,1)} %get-tuple-element.12), channel_id=1, source_target_pairs={{0,64},{8,72},{16,80},{24,88},{32,96},{40,104},{48,112},{56,120},{... | collective-permute-start | bytes 393224 | tf_op jit(solution)/shard_map/ppermute | solution.py:306
  54.7 0.9 collective-permute-start.7
  55.5 35.5 %collective-permute-done.3 = bf16[4,128,128]{2,1,0:T(8,128)(2,1)S(1)} collective-permute-done((bf16[4,128,128]{2,1,0:T(8,128)(2,1)S(1)}, bf16[4,128,128]{2,1,0:T(8,128)(2,1)S(1)}, u32[]{:S(2)}, u32[]{:S(2)}) %collective-permute-start.3) | collective-permute-done | bytes 131104 | tf_op jit(solution)/shard_map/ppermute | solution.py:306
  91.0 4.6 %collective-permute-start.8 = (bf16[4,128,128]{2,1,0:T(8,128)(2,1)S(1)}, bf16[4,128,128]{2,1,0:T(8,128)(2,1)S(1)}, u32[]{:S(2)}, u32[]{:S(2)}) collective-permute-start(bf16[4,128,128]{2,1,0:T(8,128)(2,1)S(1)} %get-tuple-element.10), channel_id=1, source_target_pairs={{0,96},{8,104},{16,112},{24,120},{32,64},{40,72},{48,80},{56,88},{... | collective-permute-start | bytes 393224 | tf_op jit(solution)/shard_map/ppermute | solution.py:306
  95.6 0.0 collective-permute-done.4
  95.6 7.2 %collective-permute-start.9 = (bf16[4,128,128]{2,1,0:T(8,128)(2,1)S(1)}, bf16[4,128,128]{2,1,0:T(8,128)(2,1)S(1)}, u32[]{:S(2)}, u32[]{:S(2)}) collective-permute-start(bf16[4,128,128]{2,1,0:T(8,128)(2,1)S(1)} %get-tuple-element.9), channel_id=1, source_target_pairs={{0,112},{8,120},{16,96},{24,104},{32,80},{40,88},{48,64},{56,72},{... | collective-permute-start | bytes 393224 | tf_op jit(solution)/shard_map/ppermute | solution.py:306
  102.8 0.3 fusion
  103.1 0.0 all-to-all-done
  103.1 0.0 copy-done.4
  103.1 21.5 %shard_map.101 = (bf16[4096,128]{1,0:T(8,128)(2,1)S(1)}, f32[16,128]{1,0:T(8,128)S(1)}) custom-call(s32[64]{0:T(128)S(1)} %copy-done.3, s32[16]{0:T(128)S(1)} %bitcast.56, bf16[192,64,128]{2,1,0:T(8,128)(2,1)} %bitcast.4.qkv, f32[16,128]{1,0:T(8,128)S(1)} %fusion.2.gate), custom_call_target="tpu_custom_call" | custom-call | tf_op jit(solution)/shard_map/pallas_call | solution.py:216
  124.7 0.0 collective-permute-done.5
  124.7 0.0 collective-permute-done.6
  124.7 0.0 collective-permute-done.7
  124.7 0.0 collective-permute-done.8
  124.7 0.0 collective-permute-done.9
  124.7 1.5 %shard_map.103 = f32[8,16,128]{2,1,0:T(8,128)} custom-call(s32[64]{0:T(128)S(1)} %select_reduce_fusion.1.when, bf16[4096,128]{1,0:T(8,128)(2,1)S(1)} %get-tuple-element.7.attn, f32[16,128]{1,0:T(8,128)S(1)} %get-tuple-element.8.square, bf16[8,64,128]{2,1,0:T(8,128)(2,1)S(1)} %bitcast.47, bf16[8,64,128]{2,1,0:T(8,128)(2,1)S(1)} %bitcast.49, ...), custom_call_target="tpu_custom_call" | custom-call | tf_op jit(solution)/shard_map/pallas_call | solution.py:262
  126.3 4.2 %all-to-all-start.1 = ((f32[8,16,128]{2,1,0:T(8,128)}), f32[8,16,128]{2,1,0:T(8,128)S(1)}, u32[]{:S(2)}, u32[]{:S(2)}) async-start(f32[8,16,128]{2,1,0:T(8,128)} %shard_map.103), calls=%async_computation.1 | async-start | bytes 131072 | tf_op jit(solution)/shard_map/all_to_all | solution.py:301
  130.4 6.3 %all-to-all-done.1 = f32[8,16,128]{2,1,0:T(8,128)S(1)} async-done(((f32[8,16,128]{2,1,0:T(8,128)}), f32[8,16,128]{2,1,0:T(8,128)S(1)}, u32[]{:S(2)}, u32[]{:S(2)}) %all-to-all-start.1) | async-done | bytes 65568 | tf_op jit(solution)/shard_map/all_to_all | solution.py:301
  136.8 1.0 shard_map.104
  (10 shorter events, 0.1 us)
Async XLA Ops:
  0.0 22.9 %copy-start = (bf16[4096,256]{1,0:T(8,128)(2,1)S(1)}, bf16[4096,256]{1,0:T(8,128)(2,1)}, u32[]{:S(2)}) copy-start(bf16[4096,256]{1,0:T(8,128)(2,1)} %param.16) | copy-start | bytes 6291460
  3.5 99.6 %all-to-all-start = ((bf16[32,384,128]{2,1,0:T(8,128)(2,1)}), bf16[32,384,128]{2,1,0:T(8,128)(2,1)}, u32[]{:S(2)}, u32[]{:S(2)}) async-start(bf16[32,384,128]{2,1,0:T(8,128)(2,1)} %shard_map.100), calls=%async_computation | async-start | bytes 6291456 | tf_op jit(solution)/shard_map/all_to_all | solution.py:301
  14.0 1.2 copy-start.1
  15.2 1.2 copy-start.2
  16.4 4.8 %copy-start.5 = (f32[1,16]{1,0:T(1,128)S(1)}, f32[1,16]{1,0:T(1,128)}, u32[]{:S(2)}) copy-start(f32[1,16]{1,0:T(1,128)} %param.15) | copy-start | bytes 196
  16.4 6.6 %copy-start.6 = (s32[64]{0:T(128)S(1)}, s32[64]{0:T(128)}, u32[]{:S(2)}) copy-start(s32[64]{0:T(128)} %constant.60.clone) | copy-start | bytes 772
  16.4 6.6 %copy-start.3 = (s32[64]{0:T(128)S(1)}, s32[64]{0:T(128)}, u32[]{:S(2)}) copy-start(s32[64]{0:T(128)} %order.1) | copy-start | bytes 772
  17.9 25.5 %collective-permute-start.2 = (bf16[8,128,128]{2,1,0:T(8,128)(2,1)}, bf16[8,128,128]{2,1,0:T(8,128)(2,1)S(1)}, u32[]{:S(2)}, u32[]{:S(2)}) collective-permute-start(bf16[8,128,128]{2,1,0:T(8,128)(2,1)} %get-tuple-element.18), channel_id=1, source_target_pairs={{0,136},{8,128},{16,152},{24,144},{32,168},{40,160},{48,184},{56,1... | collective-permute-start | bytes 786440 | tf_op jit(solution)/shard_map/ppermute | solution.py:306
  20.6 22.8 %collective-permute-start.1 = (bf16[8,128,128]{2,1,0:T(8,128)(2,1)}, bf16[8,128,128]{2,1,0:T(8,128)(2,1)S(1)}, u32[]{:S(2)}, u32[]{:S(2)}) collective-permute-start(bf16[8,128,128]{2,1,0:T(8,128)(2,1)} %get-tuple-element.19), channel_id=1, source_target_pairs={{0,128},{8,136},{16,144},{24,152},{32,160},{40,168},{48,176},{56,1... | collective-permute-start | bytes 786440 | tf_op jit(solution)/shard_map/ppermute | solution.py:306
  21.1 22.3 %collective-permute-start = (bf16[8,128,128]{2,1,0:T(8,128)(2,1)}, bf16[8,128,128]{2,1,0:T(8,128)(2,1)S(1)}, u32[]{:S(2)}, u32[]{:S(2)}) collective-permute-start(bf16[8,128,128]{2,1,0:T(8,128)(2,1)} %get-tuple-element.20), channel_id=1, source_target_pairs={{0,8},{8,0},{16,24},{24,16},{32,40},{40,32},{48,56},{56,48},{64,72... | collective-permute-start | bytes 786440 | tf_op jit(solution)/shard_map/ppermute | solution.py:306
  21.2 3.6 %collective-permute-start.10 = (f32[1,16]{1,0:T(1,128)S(1)}, f32[1,16]{1,0:T(1,128)S(1)}, u32[]{:S(2)}, u32[]{:S(2)}) collective-permute-start(f32[1,16]{1,0:T(1,128)S(1)} %copy-done.5), channel_id=1, source_target_pairs={{0,1},{1,0},{2,3},{3,2},{4,5},{5,4},{6,7},{7,6},{8,9},{9,8},{10,11... | collective-permute-start | bytes 200 | tf_op jit(solution)/shard_map/ppermute | solution.py:306
  24.8 5.2 %collective-permute-start.11 = (f32[2,16]{1,0:T(2,128)S(1)}, f32[2,16]{1,0:T(2,128)S(1)}, u32[]{:S(2)}, u32[]{:S(2)}) collective-permute-start(f32[2,16]{1,0:T(2,128)S(1)} %pad_maximum_fusion.3), channel_id=1, source_target_pairs={{0,2},{1,3},{2,0},{3,1},{4,6},{5,7},{6,4},{7,5},{8,10},{9,11},{10,... | collective-permute-start | bytes 392 | tf_op jit(solution)/shard_map/ppermute | solution.py:306
  30.0 13.3 %collective-permute-start.12 = (f32[4,16]{1,0:T(4,128)S(1)}, f32[4,16]{1,0:T(4,128)S(1)}, u32[]{:S(2)}, u32[]{:S(2)}) collective-permute-start(f32[4,16]{1,0:T(4,128)S(1)} %pad_maximum_fusion.2), channel_id=1, source_target_pairs={{0,4},{1,5},{2,6},{3,7},{4,0},{5,1},{6,2},{7,3},{8,12},{9,13},{10,... | collective-permute-start | bytes 776 | tf_op jit(solution)/shard_map/ppermute | solution.py:306
  43.4 59.7 %copy-start.4 = (s32[1,16]{1,0:T(1,128)S(1)}, s32[1,16]{1,0:T(1,128)}, u32[]{:S(2)}) copy-start(s32[1,16]{1,0:T(1,128)} %param.18) | copy-start | bytes 196
  44.3 46.7 %collective-permute-start.3 = (bf16[4,128,128]{2,1,0:T(8,128)(2,1)S(1)}, bf16[4,128,128]{2,1,0:T(8,128)(2,1)S(1)}, u32[]{:S(2)}, u32[]{:S(2)}) collective-permute-start(bf16[4,128,128]{2,1,0:T(8,128)(2,1)S(1)} %get-tuple-element.15), channel_id=1, source_target_pairs={{0,16},{8,24},{16,0},{24,8},{32,48},{40,56},{48,32},{56,40},{64,80... | collective-permute-start | bytes 393224 | tf_op jit(solution)/shard_map/ppermute | solution.py:306
  45.5 50.1 %collective-permute-start.4 = (bf16[4,128,128]{2,1,0:T(8,128)(2,1)S(1)}, bf16[4,128,128]{2,1,0:T(8,128)(2,1)S(1)}, u32[]{:S(2)}, u32[]{:S(2)}) collective-permute-start(bf16[4,128,128]{2,1,0:T(8,128)(2,1)S(1)} %get-tuple-element.14), channel_id=1, source_target_pairs={{0,32},{8,40},{16,48},{24,56},{32,0},{40,8},{48,16},{56,24},{64,96... | collective-permute-start | bytes 393224 | tf_op jit(solution)/shard_map/ppermute | solution.py:306
  48.9 75.8 %collective-permute-start.5 = (bf16[4,128,128]{2,1,0:T(8,128)(2,1)}, bf16[4,128,128]{2,1,0:T(8,128)(2,1)S(1)}, u32[]{:S(2)}, u32[]{:S(2)}) collective-permute-start(bf16[4,128,128]{2,1,0:T(8,128)(2,1)} %get-tuple-element.13), channel_id=1, source_target_pairs={{0,48},{8,56},{16,32},{24,40},{32,16},{40,24},{48,0},{56,8},{64,11... | collective-permute-start | bytes 393224 | tf_op jit(solution)/shard_map/ppermute | solution.py:306
  50.4 74.3 %collective-permute-start.6 = (bf16[4,128,128]{2,1,0:T(8,128)(2,1)}, bf16[4,128,128]{2,1,0:T(8,128)(2,1)S(1)}, u32[]{:S(2)}, u32[]{:S(2)}) collective-permute-start(bf16[4,128,128]{2,1,0:T(8,128)(2,1)} %get-tuple-element.12), channel_id=1, source_target_pairs={{0,64},{8,72},{16,80},{24,88},{32,96},{40,104},{48,112},{56,120},{... | collective-permute-start | bytes 393224 | tf_op jit(solution)/shard_map/ppermute | solution.py:306
  54.7 70.0 %collective-permute-start.7 = (bf16[4,128,128]{2,1,0:T(8,128)(2,1)}, bf16[4,128,128]{2,1,0:T(8,128)(2,1)S(1)}, u32[]{:S(2)}, u32[]{:S(2)}) collective-permute-start(bf16[4,128,128]{2,1,0:T(8,128)(2,1)} %get-tuple-element.11), channel_id=1, source_target_pairs={{0,80},{8,88},{16,64},{24,72},{32,112},{40,120},{48,96},{56,104},{... | collective-permute-start | bytes 393224 | tf_op jit(solution)/shard_map/ppermute | solution.py:306
  91.0 33.7 %collective-permute-start.8 = (bf16[4,128,128]{2,1,0:T(8,128)(2,1)S(1)}, bf16[4,128,128]{2,1,0:T(8,128)(2,1)S(1)}, u32[]{:S(2)}, u32[]{:S(2)}) collective-permute-start(bf16[4,128,128]{2,1,0:T(8,128)(2,1)S(1)} %get-tuple-element.10), channel_id=1, source_target_pairs={{0,96},{8,104},{16,112},{24,120},{32,64},{40,72},{48,80},{56,88},{... | collective-permute-start | bytes 393224 | tf_op jit(solution)/shard_map/ppermute | solution.py:306
  95.6 29.1 %collective-permute-start.9 = (bf16[4,128,128]{2,1,0:T(8,128)(2,1)S(1)}, bf16[4,128,128]{2,1,0:T(8,128)(2,1)S(1)}, u32[]{:S(2)}, u32[]{:S(2)}) collective-permute-start(bf16[4,128,128]{2,1,0:T(8,128)(2,1)S(1)} %get-tuple-element.9), channel_id=1, source_target_pairs={{0,112},{8,120},{16,96},{24,104},{32,80},{40,88},{48,64},{56,72},{... | collective-permute-start | bytes 393224 | tf_op jit(solution)/shard_map/ppermute | solution.py:306
  126.3 10.5 %all-to-all-start.1 = ((f32[8,16,128]{2,1,0:T(8,128)}), f32[8,16,128]{2,1,0:T(8,128)S(1)}, u32[]{:S(2)}, u32[]{:S(2)}) async-start(f32[8,16,128]{2,1,0:T(8,128)} %shard_map.103), calls=%async_computation.1 | async-start | bytes 131072 | tf_op jit(solution)/shard_map/all_to_all | solution.py:301
